TPU v7x, 128 devices: a whole 4x4x4 slice. The times are simulated.
128 devices in a mesh: dp: 1, ep2: 2 (over core), ep: 64 (over z, y, x).
Axes of the slice: x: 4, y: 4, z: 4, core: 2. Of those that a mesh axis runs over, the one named last changes fastest.
Arguments:
- x_tok: bfloat16 [32768, 2048], P(('dp', 'ep2', 'ep'))
- expert_ids: int32 [32768, 8], P(('dp', 'ep2', 'ep'))
- gate_w: float32 [32768, 8], P(('dp', 'ep2', 'ep'))
- w_in: bfloat16 [256, 2048, 512], P(('ep2', 'ep'))
- w_out: bfloat16 [256, 512, 2048], P(('ep2', 'ep'))
Outputs:
- output: bfloat16 [32768, 2048], P(('dp', 'ep2', 'ep'))
All inputs are finite; a program needn't handle non-finite values.
Results may differ from a plain program's by a relative error of at most 0.00101.
Values are sent between devices in bfloat16 or wider.
A program may use at most 1 GiB of HBM per device.

v0:
```python
import jax
import jax.numpy as jnp
from jax import lax
from jax.sharding import PartitionSpec as P


def slot_sizes(group_size, n_tok, n_top, experts):
    capacity = 8 * ((5 * group_size * n_tok * n_top) // (32 * experts))
    lane_max = 2 * ((n_tok * n_top) // experts) - 1
    return capacity, lane_max


def pack_rows(x_loc, flat_e, counts, offsets, capacity, lane_max):
    n_tok = x_loc.shape[0]
    n_pair = flat_e.shape[0]
    pair_order = jnp.argsort(flat_e, stable=True)
    starts = jnp.cumsum(counts) - counts
    kept_n = jnp.clip(capacity - offsets, 0, counts)
    lane_ids = jnp.arange(lane_max)
    src_pair = pair_order[jnp.minimum(starts[:, None] + lane_ids[None, :], n_pair - 1)]
    is_kept = lane_ids[None, :] < kept_n[:, None]
    send_rows = jnp.where(is_kept[:, :, None], x_loc[src_pair // (n_pair // n_tok)], jnp.zeros((), x_loc.dtype))
    sorted_rank = jnp.arange(n_pair) - starts[flat_e[pair_order]]
    pair_rank = jnp.zeros((n_pair,), jnp.int32).at[pair_order].set(sorted_rank)
    return send_rows, pair_rank, kept_n


def expert_rows(recv_rows, src_counts, src_offsets, w_a, w_b, capacity):
    group_size, e_loc, lane_max, d_model = recv_rows.shape
    range_end = src_offsets + src_counts
    totals = jnp.sum(src_counts, axis=0)
    slot_ids = jnp.arange(capacity)
    src_dev = jnp.sum((range_end[:, :, None] <= slot_ids[None, None, :]).astype(jnp.int32), axis=0)
    src_dev = jnp.minimum(src_dev, group_size - 1)
    expert_pos = jnp.arange(e_loc)[:, None]
    slot_base = jnp.take_along_axis(src_offsets.T, src_dev, axis=1)
    lane_pos = jnp.clip(slot_ids[None, :] - slot_base, 0, lane_max - 1)
    flat_pos = (src_dev * e_loc + expert_pos) * lane_max + lane_pos
    filled = slot_ids[None, :] < totals[:, None]
    gathered = recv_rows.reshape(group_size * e_loc * lane_max, d_model)[flat_pos]
    slot_rows = jnp.where(filled[:, :, None], gathered, jnp.zeros((), recv_rows.dtype))
    hidden = jax.nn.gelu(jnp.einsum('ecd,edf->ecf', slot_rows, w_a, preferred_element_type=jnp.float32), approximate=True).astype(jnp.bfloat16)
    out_rows = jnp.einsum('ecf,efd->ecd', hidden, w_b, preferred_element_type=jnp.float32).astype(jnp.bfloat16)
    back_pos = expert_pos[None] * capacity + jnp.clip(src_offsets[:, :, None] + jnp.arange(lane_max)[None, None, :], 0, capacity - 1)
    return out_rows.reshape(e_loc * capacity, d_model)[back_pos]


def combine_rows(x_loc, back_rows, flat_e, flat_gate, pair_rank, kept_n):
    n_tok, d_model = x_loc.shape
    experts, lane_max, _ = back_rows.shape
    n_top = flat_e.shape[0] // n_tok
    got_rows = back_rows.reshape(experts * lane_max, d_model)[flat_e * lane_max + pair_rank]
    weight = jnp.where(pair_rank < kept_n[flat_e], flat_gate, 0.0)
    mix_sum = jnp.sum((weight[:, None] * got_rows.astype(jnp.float32)).reshape(n_tok, n_top, d_model), axis=1)
    return (x_loc.astype(jnp.float32) + mix_sum).astype(jnp.bfloat16)


def solution(mesh):
    dev_axes = ('ep2', 'ep')
    group_size = mesh.shape['ep2'] * mesh.shape['ep']

    def local_step(x_loc, ids_loc, gate_loc, w_a, w_b):
        n_tok, d_model = x_loc.shape
        n_top = ids_loc.shape[1]
        e_loc = w_a.shape[0]
        experts = e_loc * group_size
        capacity, lane_max = slot_sizes(group_size, n_tok, n_top, experts)
        flat_e = ids_loc.reshape(-1)
        counts = jnp.bincount(flat_e, length=experts)
        src_counts = lax.all_to_all(counts.reshape(group_size, e_loc), dev_axes, 0, 0, tiled=True)
        src_offsets = jnp.cumsum(src_counts, axis=0) - src_counts
        offsets = lax.all_to_all(src_offsets, dev_axes, 0, 0, tiled=True).reshape(experts)
        send_rows, pair_rank, kept_n = pack_rows(x_loc, flat_e, counts, offsets, capacity, lane_max)
        recv_rows = lax.all_to_all(send_rows.reshape(group_size, e_loc, lane_max, d_model), dev_axes, 0, 0, tiled=True)
        out_rows = expert_rows(recv_rows, src_counts, src_offsets, w_a, w_b, capacity)
        back_rows = lax.all_to_all(out_rows, dev_axes, 0, 0, tiled=True).reshape(experts, lane_max, d_model)
        return combine_rows(x_loc, back_rows, flat_e, gate_loc.reshape(-1), pair_rank, kept_n)

    tok_spec = P(('dp', 'ep2', 'ep'), None)
    w_spec = P(dev_axes, None, None)
    return jax.shard_map(local_step, mesh=mesh, in_specs=(tok_spec, tok_spec, tok_spec, w_spec, w_spec), out_specs=tok_spec, check_vma=False)
```

profile of v0, /device:TPU:8, one launch (start us, length us, event | category | flops | bytes accessed | tf_op | source)
XLA Modules:
  0.0 892.4 jit_solution(9630176232973151947)
XLA Ops:
  1.6 14.7 %scatter_custom_fusion = s32[256]{0:T(256)S(1)} fusion(s32[2048]{0:T(1024)S(1)} %bitcast.53, s32[2048]{0:T(1024)S(1)} %broadcast.389, s32[]{:T(128)} %constant.24.clone.1), kind=kCustom, calls=%fused_computation.74 | custom fusion | flops 2048 | bytes 1028 | tf_op jit(solution)/shard_map/scatter-add | solution.py:69
  17.0 10.4 %all-to-all-start = ((s32[128,1,2]{2,1,0:T(1,128)}), s32[128,1,2]{2,1,0:T(1,128)S(1)}, u32[]{:S(2)}, u32[]{:S(2)}) async-start(s32[128,1,2]{2,1,0:T(1,128)} %bitcast.5), calls=%async_computation | async-start | bytes 131072 | tf_op jit(solution)/shard_map/all_to_all | solution.py:70
  52.8 20.2 %gather_fusion.3 = s32[3840]{0:T(1024)S(1)} fusion(s32[2048]{0:T(1024)S(1)} %get-tuple-element.6, s32[4096]{0:T(1024)S(1)} %pad_clamp_fusion.2), kind=kCustom, calls=%fused_computation.3 | custom fusion | bytes 46080 | tf_op jit(solution)/shard_map/gather | solution.py:20
  73.5 15.6 %gather_fusion.4 = bf16[3840,2048]{1,0:T(8,128)(2,1)} fusion(bf16[256,2048]{1,0:T(8,128)(2,1)S(1)} %copy-done.6, s32[4096]{0:T(1024)S(1)} %pad_clamp_fusion.1), kind=kCustom, calls=%fused_computation.4 | custom fusion | bytes 31472640 | tf_op jit(solution)/shard_map/gather | solution.py:22
  89.1 18.6 %gather.43 = bf16[128,2,15,2048]{3,2,1,0:T(8,128)(2,1)} reshape(bf16[3840,2048]{1,0:T(8,128)(2,1)} %gather_fusion.4) | data formatting | bytes 31457280 | tf_op jit(solution)/shard_map/gather | solution.py:22
  116.3 38.3 %copy.37 = bf16[128,2,15,2048]{3,1,2,0:T(2,128)(2,1)} copy(bf16[128,2,15,2048]{3,2,1,0:T(8,128)(2,1)S(1)} %broadcast_select_fusion) | data formatting | bytes 31457280 | tf_op jit(solution)/shard_map/jit(_where)/select_n | solution.py:22
  162.2 17.4 %gather_fusion.8 = s32[2560]{0:T(1024)S(1)} fusion(s32[2,128]{0,1:T(8,128)S(1)} %bitcast.44, s32[2560]{0:T(1024)S(1)} %reshape.442), kind=kCustom, calls=%fused_computation.8 | custom fusion | bytes 40960 | tf_op jit(solution)/shard_map/jit(take_along_axis)/gather | solution.py:36
  180.4 203.3 %all-to-all-done.2 = bf16[128,2,15,2048]{3,1,2,0:T(2,128)(2,1)} async-done(((bf16[128,2,15,2048]{3,1,2,0:T(2,128)(2,1)}), bf16[128,2,15,2048]{3,1,2,0:T(2,128)(2,1)}, u32[]{:S(2)}, u32[]{:S(2)}) %all-to-all-start.2) | async-done | bytes 15728672 | tf_op jit(solution)/shard_map/all_to_all | solution.py:74
  383.7 16.8 %copy.38 = bf16[128,2,15,2048]{3,2,1,0:T(8,128)(2,1)} copy(bf16[128,2,15,2048]{3,1,2,0:T(2,128)(2,1)} %all-to-all-done.2) | data formatting | bytes 31457280 | tf_op jit(solution)/shard_map/all_to_all | solution.py:74
  400.6 18.7 %reshape.375 = bf16[3840,2048]{1,0:T(8,128)(2,1)} reshape(bf16[128,2,15,2048]{3,2,1,0:T(8,128)(2,1)} %copy.38) | data formatting | bytes 31457280 | tf_op jit(solution)/shard_map/reshape | solution.py:40
  419.3 27.6 %gather_fusion.5 = bf16[2560,2048]{1,0:T(8,128)(2,1)} fusion(bf16[3840,2048]{1,0:T(8,128)(2,1)} %reshape.375, s32[3072]{0:T(1024)S(1)} %pad_clamp_fusion.3), kind=kCustom, calls=%fused_computation.5 | custom fusion | bytes 20981760 | tf_op jit(solution)/shard_map/gather | solution.py:40
  446.9 18.4 %convolution_convert_fusion = bf16[2,1280,2048]{2,1,0:T(8,128)(2,1)} fusion(bf16[2,512,2048]{2,1,0:T(8,128)(2,1)} %param.9, bf16[2,2048,512]{2,1,0:T(8,128)(2,1)} %param.8, bf16[2,1280,2048]{2,1,0:T(8,128)(2,1)} %bitcast.46, pred[2,1280]{1,0:T(4,128)(4,1)S(1)} %iota_compare_fusion.2), kind=kOutput, calls=%fused_computation.14 | convolution fusion | flops 10759700480 | bytes 29362688 | tf_op jit(solution)/shard_map/ecf,efd->ecd/dot_general | solution.py:43
  465.3 34.8 %gather_fusion.6 = bf16[3840,2048]{1,0:T(8,128)(2,1)} fusion(bf16[2560,2048]{1,0:T(8,128)(2,1)} %bitcast.45, s32[4096]{0:T(1024)S(1)} %pad_clamp_fusion), kind=kCustom, calls=%fused_computation.6 | custom fusion | bytes 31472640 | tf_op jit(solution)/shard_map/gather | solution.py:45
  500.1 18.6 %reshape.427 = bf16[128,2,15,2048]{3,2,1,0:T(8,128)(2,1)} reshape(bf16[3840,2048]{1,0:T(8,128)(2,1)} %gather_fusion.6) | data formatting | bytes 31457280 | tf_op jit(solution)/shard_map/gather | solution.py:45
  518.7 30.4 %copy.40 = bf16[128,2,15,2048]{3,1,2,0:T(2,128)(2,1)} copy(bf16[128,2,15,2048]{3,2,1,0:T(8,128)(2,1)} %reshape.427) | data formatting | bytes 31457280 | tf_op jit(solution)/shard_map/gather | solution.py:45
  549.1 33.1 %all-to-all-start.3 = ((bf16[128,2,15,2048]{3,1,2,0:T(2,128)(2,1)}), bf16[128,2,15,2048]{3,1,2,0:T(2,128)(2,1)}, u32[]{:S(2)}, u32[]{:S(2)}) async-start(bf16[128,2,15,2048]{3,1,2,0:T(2,128)(2,1)} %copy.40), calls=%async_computation.3 | async-start | bytes 31457280 | tf_op jit(solution)/shard_map/all_to_all | solution.py:76
  582.3 11.8 %gather_fusion = s32[2048]{0:T(1024)S(1)} fusion(s32[2048]{0:T(1024)S(1)} %copy-done.9, s32[2048]{0:T(1024)S(1)} %get-tuple-element.9), kind=kCustom, calls=%fused_computation | custom fusion | bytes 24576 | tf_op jit(solution)/shard_map/gather | solution.py:23
  594.4 13.1 %gather_fusion.1 = s32[2048]{0:T(1024)S(1)} fusion(s32[256]{0:T(256)S(1)} %copy-done.5, s32[2048]{0:T(1024)S(1)} %broadcast_clamp_fusion.1), kind=kCustom, calls=%fused_computation.1 | custom fusion | bytes 24576 | tf_op jit(solution)/shard_map/gather | solution.py:23
  607.6 13.1 %gather_fusion.2 = s32[2048]{0:T(1024)S(1)} fusion(s32[256]{0:T(256)S(1)} %copy-done.3, s32[2048]{0:T(1024)S(1)} %broadcast_clamp_fusion), kind=kCustom, calls=%fused_computation.2 | custom fusion | bytes 24576 | tf_op jit(solution)/shard_map/gather | solution.py:53
  628.9 191.1 %all-to-all-done.3 = bf16[128,2,15,2048]{3,1,2,0:T(2,128)(2,1)} async-done(((bf16[128,2,15,2048]{3,1,2,0:T(2,128)(2,1)}), bf16[128,2,15,2048]{3,1,2,0:T(2,128)(2,1)}, u32[]{:S(2)}, u32[]{:S(2)}) %all-to-all-start.3) | async-done | bytes 15728672 | tf_op jit(solution)/shard_map/all_to_all | solution.py:76
  820.0 16.8 %copy.41 = bf16[128,2,15,2048]{3,2,1,0:T(8,128)(2,1)} copy(bf16[128,2,15,2048]{3,1,2,0:T(2,128)(2,1)} %all-to-all-done.3) | data formatting | bytes 31457280 | tf_op jit(solution)/shard_map/all_to_all | solution.py:76
  836.9 18.7 %reshape_reshape.3 = bf16[3840,2048]{1,0:T(8,128)(2,1)} reshape(bf16[128,2,15,2048]{3,2,1,0:T(8,128)(2,1)} %copy.41) | data formatting | bytes 31457280 | tf_op jit(solution)/shard_map/reshape;reshape | solution.py:52
  855.5 24.1 %gather_fusion.7 = bf16[2048,2048]{1,0:T(8,128)(2,1)} fusion(bf16[3840,2048]{1,0:T(8,128)(2,1)} %reshape_reshape.3, s32[2048]{0:T(1024)S(1)} %fusion.25), kind=kCustom, calls=%fused_computation.7 | custom fusion | bytes 16785408 | tf_op jit(solution)/shard_map/gather | solution.py:52
  879.6 11.2 %fusion = f32[256,2048]{1,0:T(8,128)S(1)} fusion(bf16[2048,2048]{1,0:T(8,128)(2,1)} %gather_fusion.7, f32[256,8]{1,0:T(8,128)S(1)} %mul.72), kind=kLoop, calls=%fused_computation.12 | loop fusion | flops 12058624 | bytes 10493952 | tf_op jit(solution)/shard_map/reduce_sum | solution.py:54
  (84 shorter events, 54.7 us)
Async XLA Ops:
  17.0 19.4 %all-to-all-start = ((s32[128,1,2]{2,1,0:T(1,128)}), s32[128,1,2]{2,1,0:T(1,128)S(1)}, u32[]{:S(2)}, u32[]{:S(2)}) async-start(s32[128,1,2]{2,1,0:T(1,128)} %bitcast.5), calls=%async_computation | async-start | bytes 131072 | tf_op jit(solution)/shard_map/all_to_all | solution.py:70
  37.5 14.0 %all-to-all-start.1 = ((s32[128,1,2]{2,1,0:T(1,128)}), s32[128,1,2]{2,1,0:T(1,128)S(1)}, u32[]{:S(2)}, u32[]{:S(2)}) async-start(s32[128,1,2]{2,1,0:T(1,128)} %copy.35), calls=%async_computation.1 | async-start | bytes 131072 | tf_op jit(solution)/shard_map/all_to_all | solution.py:72
  42.7 9.0 %copy-start.8 = (s32[2048]{0:T(1024)}, s32[2048]{0:T(1024)S(1)}, u32[]{:S(2)}) copy-start(s32[2048]{0:T(1024)S(1)} %reshape.370) | copy-start | bytes 24580
  47.7 25.3 %copy-start = (s32[2048]{0:T(1024)}, s32[2048]{0:T(1024)S(1)}, u32[]{:S(2)}) copy-start(s32[2048]{0:T(1024)S(1)} %get-tuple-element.6) | copy-start | bytes 24580
  51.9 0.6 copy-start.4
  51.9 55.7 %copy-start.2 = (s32[256]{0:T(256)}, s32[256]{0:T(256)S(1)}, u32[]{:S(2)}) copy-start(s32[256]{0:T(256)S(1)} %get-tuple-element.11) | copy-start | bytes 3076
  52.8 20.7 %copy-start.6 = (bf16[256,2048]{1,0:T(8,128)(2,1)S(1)}, bf16[256,2048]{1,0:T(8,128)(2,1)}, u32[]{:S(2)}) copy-start(bf16[256,2048]{1,0:T(8,128)(2,1)} %param.5) | copy-start | bytes 3145732
  154.6 229.1 %all-to-all-start.2 = ((bf16[128,2,15,2048]{3,1,2,0:T(2,128)(2,1)}), bf16[128,2,15,2048]{3,1,2,0:T(2,128)(2,1)}, u32[]{:S(2)}, u32[]{:S(2)}) async-start(bf16[128,2,15,2048]{3,1,2,0:T(2,128)(2,1)} %copy.37), calls=%async_computation.2 | async-start | bytes 31457280 | tf_op jit(solution)/shard_map/all_to_all | solution.py:74
  549.1 33.1 %copy-start.1 = (s32[2048]{0:T(1024)S(1)}, s32[2048]{0:T(1024)}, u32[]{:S(2)}) copy-start(s32[2048]{0:T(1024)} %copy-done) | copy-start | bytes 24580
  549.1 33.2 %copy-start.9 = (s32[2048]{0:T(1024)S(1)}, s32[2048]{0:T(1024)}, u32[]{:S(2)}) copy-start(s32[2048]{0:T(1024)} %copy-done.8) | copy-start | bytes 24580
  549.1 270.9 %all-to-all-start.3 = ((bf16[128,2,15,2048]{3,1,2,0:T(2,128)(2,1)}), bf16[128,2,15,2048]{3,1,2,0:T(2,128)(2,1)}, u32[]{:S(2)}, u32[]{:S(2)}) async-start(bf16[128,2,15,2048]{3,1,2,0:T(2,128)(2,1)} %copy.40), calls=%async_computation.3 | async-start | bytes 31457280 | tf_op jit(solution)/shard_map/all_to_all | solution.py:76
  582.3 11.9 %copy-start.11 = (f32[256,8]{0,1:T(8,128)S(1)}, f32[256,8]{0,1:T(8,128)}, u32[]{:S(2)}) copy-start(f32[256,8]{0,1:T(8,128)} %param.7) | copy-start | bytes 24580
  582.3 12.1 %copy-start.10 = (s32[2048,1]{0,1:T(1,128)S(1)}, s32[2048,1]{0,1:T(1,128)}, u32[]{:S(2)}) copy-start(s32[2048,1]{0,1:T(1,128)} %get-tuple-element.7) | copy-start | bytes 24580
  582.3 12.1 %copy-start.5 = (s32[256]{0:T(256)S(1)}, s32[256]{0:T(256)}, u32[]{:S(2)}) copy-start(s32[256]{0:T(256)} %copy-done.4) | copy-start | bytes 3076
  582.3 25.3 %copy-start.3 = (s32[256]{0:T(256)S(1)}, s32[256]{0:T(256)}, u32[]{:S(2)}) copy-start(s32[256]{0:T(256)} %copy-done.2) | copy-start | bytes 3076
  879.6 11.3 %copy-start.7 = (bf16[256,2048]{1,0:T(8,128)(2,1)S(1)}, bf16[256,2048]{1,0:T(8,128)(2,1)}, u32[]{:S(2)}) copy-start(bf16[256,2048]{1,0:T(8,128)(2,1)} %param.5) | copy-start | bytes 3145732
where the time goes:
time: 901 us; the launch traced here: 892 us
  waiting for transfers between devices  407 us (45%)
  local copies, waits for them, and re-layouts  368 us (41%)
  starting transfers between devices  55.8 us (6%)
  other arithmetic  43.1 us (5%)
  matrix products  18.4 us (2%)
    all_to_all x1, waiting for transfers between devices, local_step(): lax.all_to_all(send_rows.reshape(group_size, e_loc, lane_max, d_model), d...  203 us
    all_to_all x1, waiting for transfers between devices, local_step(): lax.all_to_all(out_rows, dev_axes, 0, 0, tiled=True)  191 us
    gather x3, local copies, waits for them, and re-layouts, expert_rows(): return out_rows.reshape(e_loc * capacity, d_model)[back_pos]  83.8 us
    select_n x1, local copies, waits for them, and re-layouts, pack_rows(): jnp.where(is_kept[:, :, None], x_loc[src_pair // (n_pair // n_tok)], jnp....  38.3 us
    gather x2, local copies, waits for them, and re-layouts, pack_rows(): x_loc[src_pair // (n_pair // n_tok)]  34.1 us
    all_to_all x1, starting transfers between devices, local_step(): lax.all_to_all(out_rows, dev_axes, 0, 0, tiled=True)  33.1 us
    gather x1, local copies, waits for them, and re-layouts, expert_rows(): recv_rows.reshape(group_size * e_loc * lane_max, d_model)[flat_pos]  27.6 us
    gather x2, local copies, waits for them, and re-layouts, pack_rows(): sorted_rank = jnp.arange(n_pair) - starts[flat_e[pair_order]]  24.9 us
  transfers between devices with their start and end apart: 4, of which 4 were waited for; matrix products, arithmetic and copies ran while one was open for 8% of the time, Pallas kernels for 0%

commit v1 on v0

v1 whole, which is shorter than its diff:
```python
import functools

import jax
import jax.numpy as jnp
from jax import lax
from jax.experimental import pallas as pl
from jax.experimental.pallas import tpu as pltpu
from jax.sharding import PartitionSpec as P

LANES = 16


def onehot_sum(keys, values, width, base=0):
    n_tok, n_top = keys.shape
    cols = lax.broadcasted_iota(jnp.int32, (n_tok, width), 1) + base
    total = jnp.zeros((n_tok, width), jnp.float32)
    for j in range(n_top):
        total = jnp.where(cols == keys[:, j:j + 1], values[j], total)
    return total


def route_kernel(ids_ref, slot_ref, count_ref):
    ids = ids_ref[...]
    n_tok, n_top = ids.shape
    experts = count_ref.shape[1]
    member = onehot_sum(ids, [1.0] * n_top, experts)
    row = lax.broadcasted_iota(jnp.int32, (n_tok, n_tok), 0)
    col = lax.broadcasted_iota(jnp.int32, (n_tok, n_tok), 1)
    earlier = jnp.where(col < row, 1.0, 0.0).astype(jnp.bfloat16)
    before = jnp.dot(earlier, member.astype(jnp.bfloat16), preferred_element_type=jnp.float32)
    count_ref[...] = jnp.sum(member, axis=0, keepdims=True).astype(jnp.int32)
    cols = lax.broadcasted_iota(jnp.int32, (n_tok, experts), 1)
    for j in range(n_top):
        rank = jnp.sum(jnp.where(cols == ids[:, j:j + 1], before, 0.0), axis=1, keepdims=True)
        slot_ref[:, j:j + 1] = ids[:, j:j + 1] * LANES + rank.astype(jnp.int32)


def route(ids, experts):
    return pl.pallas_call(
        route_kernel,
        out_shape=(jax.ShapeDtypeStruct(ids.shape, jnp.int32), jax.ShapeDtypeStruct((1, experts), jnp.int32)),
        name='route',
    )(ids)


def pack_kernel(slot_ref, x_ref, out_ref):
    rows = out_ref.shape[0]
    pick = onehot_sum(slot_ref[...], [1.0] * slot_ref.shape[1], rows, pl.program_id(0) * rows).astype(jnp.bfloat16)
    out_ref[...] = lax.dot_general(pick, x_ref[...], (((0,), (0,)), ((), ())), preferred_element_type=jnp.float32).astype(out_ref.dtype)


def pack(slot, x, n_slot, rows=512):
    n_tok, d_model = x.shape
    return pl.pallas_call(
        pack_kernel,
        grid=(n_slot // rows,),
        in_specs=[pl.BlockSpec(slot.shape, lambda i: (0, 0)), pl.BlockSpec(x.shape, lambda i: (0, 0))],
        out_specs=pl.BlockSpec((rows, d_model), lambda i: (i, 0)),
        out_shape=jax.ShapeDtypeStruct((n_slot, d_model), x.dtype),
        cost_estimate=pl.CostEstimate(flops=2 * n_slot * n_tok * d_model, bytes_accessed=2 * n_slot * d_model, transcendentals=0),
        name='pack',
    )(slot, x)


def expert_kernel(rows_ref, w_in_ref, w_out_ref, out_ref):
    shape = rows_ref.shape
    rows = rows_ref[...].reshape(shape[0] * shape[2], shape[3])
    hidden = jax.nn.gelu(jnp.dot(rows, w_in_ref[0], preferred_element_type=jnp.float32), approximate=True).astype(jnp.bfloat16)
    out_ref[...] = jnp.dot(hidden, w_out_ref[0], preferred_element_type=jnp.float32).astype(out_ref.dtype).reshape(shape)


def expert(rows, w_in, w_out, group=32):
    n_src, e_loc, lanes, d_model = rows.shape
    ff = w_in.shape[2]
    row_spec = pl.BlockSpec((group, 1, lanes, d_model), lambda e, i: (i, e, 0, 0))
    return pl.pallas_call(
        expert_kernel,
        grid=(e_loc, n_src // group),
        in_specs=[row_spec, pl.BlockSpec((1, d_model, ff), lambda e, i: (e, 0, 0)), pl.BlockSpec((1, ff, d_model), lambda e, i: (e, 0, 0))],
        out_specs=row_spec,
        out_shape=jax.ShapeDtypeStruct(rows.shape, rows.dtype),
        compiler_params=pltpu.CompilerParams(vmem_limit_bytes=48 * 2**20),
        cost_estimate=pl.CostEstimate(flops=4 * n_src * e_loc * lanes * d_model * ff, bytes_accessed=4 * rows.size, transcendentals=0),
        name='expert',
    )(rows, w_in, w_out)


def combine_kernel(capacity, slot_ref, ids_ref, gate_ref, off_ref, x_ref, back_ref, out_ref, acc_ref, weight_ref):
    step = pl.program_id(0)
    n_tok, n_top = ids_ref.shape
    experts = off_ref.shape[1]
    rows = back_ref.shape[0]

    @pl.when(step == 0)
    def _():
        ids = ids_ref[...]
        off = off_ref[...].astype(jnp.float32)
        cols = lax.broadcasted_iota(jnp.int32, (n_tok, experts), 1)
        for j in range(n_top):
            first = jnp.sum(jnp.where(cols == ids[:, j:j + 1], off, 0.0), axis=1, keepdims=True).astype(jnp.int32)
            rank = first + slot_ref[:, j:j + 1] - ids[:, j:j + 1] * LANES
            weight_ref[:, j:j + 1] = jnp.where(rank < capacity, gate_ref[:, j:j + 1], 0.0)
        acc_ref[...] = x_ref[...].astype(jnp.float32)

    weight = weight_ref[...]
    gates = onehot_sum(slot_ref[...], [weight[:, j:j + 1] for j in range(n_top)], rows, step * rows)
    high = gates.astype(jnp.bfloat16)
    rest = gates - high.astype(jnp.float32)
    mid = rest.astype(jnp.bfloat16)
    low = (rest - mid.astype(jnp.float32)).astype(jnp.bfloat16)
    parts = jnp.concatenate([high, mid, low], axis=0)
    mix = jnp.dot(parts, back_ref[...], preferred_element_type=jnp.float32)
    acc_ref[...] += mix[:n_tok] + mix[n_tok:2 * n_tok] + mix[2 * n_tok:]

    @pl.when(step == pl.num_programs(0) - 1)
    def _():
        out_ref[...] = acc_ref[...].astype(out_ref.dtype)


def combine(slot, ids, gate, off, x, back, capacity, rows=512):
    n_tok, d_model = x.shape
    whole = lambda a: pl.BlockSpec(a.shape, lambda i: (0, 0))
    return pl.pallas_call(
        functools.partial(combine_kernel, capacity),
        grid=(back.shape[0] // rows,),
        in_specs=[whole(slot), whole(ids), whole(gate), whole(off), whole(x), pl.BlockSpec((rows, d_model), lambda i: (i, 0))],
        out_specs=whole(x),
        out_shape=jax.ShapeDtypeStruct(x.shape, x.dtype),
        scratch_shapes=[pltpu.VMEM(x.shape, jnp.float32), pltpu.VMEM(ids.shape, jnp.float32)],
        compiler_params=pltpu.CompilerParams(vmem_limit_bytes=48 * 2**20),
        name='combine',
    )(slot, ids, gate, off, x, back)


def solution(mesh):
    dev_axes = ('ep2', 'ep')
    group_size = mesh.shape['ep2'] * mesh.shape['ep']

    def local_step(x_loc, ids_loc, gate_loc, w_a, w_b):
        n_tok, d_model = x_loc.shape
        n_top = ids_loc.shape[1]
        e_loc = w_a.shape[0]
        experts = e_loc * group_size
        capacity = 8 * ((5 * group_size * n_tok * n_top) // (32 * experts))
        slot, counts = route(ids_loc, experts)
        send = pack(slot, x_loc, experts * LANES)
        recv = lax.all_to_all(send.reshape(group_size, e_loc * LANES, d_model), dev_axes, 0, 0, tiled=True)
        all_counts = lax.all_gather(counts[0], dev_axes)
        earlier = jnp.arange(group_size)[:, None] < lax.axis_index(dev_axes)
        off = jnp.sum(jnp.where(earlier, all_counts, 0), axis=0, keepdims=True)
        out = expert(recv.reshape(group_size, e_loc, LANES, d_model), w_a, w_b)
        back = lax.all_to_all(out.reshape(group_size, e_loc * LANES, d_model), dev_axes, 0, 0, tiled=True)
        return combine(slot, ids_loc, gate_loc, off, x_loc, back.reshape(experts * LANES, d_model), capacity)

    tok_spec = P(('dp', 'ep2', 'ep'), None)
    w_spec = P(dev_axes, None, None)
    return jax.shard_map(local_step, mesh=mesh, in_specs=(tok_spec, tok_spec, tok_spec, w_spec, w_spec), out_specs=tok_spec, check_vma=False)
```

time: 901 us -> 871 us (0.967)
  the two profiles are of different devices: /device:TPU:8 before, /device:TPU:1 now
where the time goes in v1:
time: 871 us
  blocking collectives  792 us (91%)
  Pallas kernels  64.2 us (7%)
  starting transfers between devices  13 us (1%)
    all_gather x1, blocking collectives, local_step(): all_counts = lax.all_gather(counts[0], dev_axes)  551 us
    all_to_all x1, blocking collectives, local_step(): lax.all_to_all(send.reshape(group_size, e_loc * LANES, d_model), dev_axes...  241 us
    pallas_call x1, Pallas kernels, expert(): pl.pallas_call(expert_kernel, grid=(e_loc, n_src // group), in_specs=[row...  24.5 us
    pallas_call x1, Pallas kernels, combine(): pl.pallas_call(functools.partial(combine_kernel, capacity), grid=(back.sh...  24.4 us
  transfers between devices with their start and end apart: 1, of which 0 were waited for; matrix products, arithmetic and copies ran while one was open for 0% of the time, Pallas kernels for 0%

profile of v1, /device:TPU:1, one launch (start us, length us, event | category | flops | bytes accessed | tf_op | source)
XLA Modules:
  0.0 870.8 jit_solution(3646537592361676762)
XLA Ops:
  0.0 1.5 copy.9.ids_ref
  1.5 2.6 route.1
  4.0 12.7 %pack.1 = bf16[4096,2048]{1,0:T(8,128)(2,1)} custom-call(s32[256,8]{1,0:T(8,128)} %get-tuple-element.7.slot_ref, bf16[256,2048]{1,0:T(8,128)(2,1)} %x_ref.3), custom_call_target="tpu_custom_call" | custom-call | flops 4294967296 | bytes 16777216 | tf_op jit(solution)/shard_map/pack/pallas_call | solution.py:54
  16.8 0.0 copy-start.3
  16.8 241.2 %all_to_all.10 = bf16[128,32,2048]{2,1,0:T(8,128)(2,1)} all-to-all(bf16[128,32,2048]{2,1,0:T(8,128)(2,1)} %bitcast.11), channel_id=1, replica_groups=mesh['dp'=1,'ep2'=2,'ep'=64] {'ep2','ep'}, dimensions={0} | all-to-all | bytes 33554432 | tf_op jit(solution)/shard_map/all_to_all | solution.py:147
  257.9 0.0 copy-done.3
  257.9 24.5 %expert.1 = bf16[128,2,16,2048]{3,2,1,0:T(8,128)(2,1)} custom-call(bf16[128,2,16,2048]{3,2,1,0:T(8,128)(2,1)} %bitcast.13, bf16[2,2048,512]{2,1,0:T(8,128)(2,1)S(1)} %copy-done.3, bf16[2,512,2048]{2,1,0:T(8,128)(2,1)} %w_out_ref.1), custom_call_target="tpu_custom_call" | custom-call | flops 17179869184 | bytes 33554432 | tf_op jit(solution)/shard_map/expert/pallas_call | solution.py:76
  282.5 0.0 copy-start.4
  282.5 0.0 copy-start.5
  282.5 0.0 copy-start
  282.5 0.0 copy-start.1
  282.5 0.0 copy-start.2
  282.5 13.0 %all-to-all-start.1 = ((bf16[128,32,2048]{2,1,0:T(8,128)(2,1)}), bf16[128,32,2048]{2,1,0:T(8,128)(2,1)}, u32[]{:S(2)}, u32[]{:S(2)}) async-start(bf16[128,32,2048]{2,1,0:T(8,128)(2,1)} %bitcast.12), calls=%async_computation.1 | async-start | bytes 33554432 | tf_op jit(solution)/shard_map/all_to_all | solution.py:152
  295.5 0.0 copy-done.4
  295.5 0.1 copy.11.gate_ref
  295.6 0.0 copy-done.5
  295.6 550.6 %all-gather = s32[128,1,256]{2,1,0:T(1,128)S(1)} all-gather(s32[1,1,256]{2,1,0:T(1,128)S(1)} %bitcast.14), channel_id=1, replica_groups=mesh['dp'=1,'ep2'=2,'ep'=64] {'ep2','ep'}, dimensions={0}, use_global_device_ids=true | all-gather | bytes 132096 | tf_op jit(solution)/shard_map/all_gather | solution.py:148
  846.3 0.1 fusion
  846.4 0.0 all-to-all-done.1
  846.4 0.0 copy-done
  846.4 0.0 copy-done.1
  846.4 0.0 copy-done.2
  846.4 24.4 %combine.1 = bf16[256,2048]{1,0:T(8,128)(2,1)} custom-call(s32[256,8]{1,0:T(8,128)S(1)} %copy-done.2, s32[256,8]{1,0:T(8,128)S(1)} %copy-done.1, f32[256,8]{1,0:T(8,128)S(1)} %copy.11.gate_ref, s32[1,256]{1,0:T(1,128)S(1)} %bitcast.10, bf16[256,2048]{1,0:T(8,128)(2,1)S(1)} %copy-done, bf16[4096,2048]{1,0:T(8,128)(2,1)} %bitcast.5.back_ref), custom_call_target="tpu_custom_call" | custom-call | tf_op jit(solution)/shard_map/combine/pallas_call | solution.py:123
  (1 shorter events, 0.0 us)
Async XLA Ops:
  16.8 241.2 %copy-start.3 = (bf16[2,2048,512]{2,1,0:T(8,128)(2,1)S(1)}, bf16[2,2048,512]{2,1,0:T(8,128)(2,1)}, u32[]{:S(2)}) copy-start(bf16[2,2048,512]{2,1,0:T(8,128)(2,1)} %w_in_ref.1) | copy-start | bytes 12582916
  282.5 13.0 %copy-start.4 = (f32[256,8]{0,1:T(8,128)S(1)}, f32[256,8]{0,1:T(8,128)}, u32[]{:S(2)}) copy-start(f32[256,8]{0,1:T(8,128)} %param.7) | copy-start | bytes 24580
  282.5 13.1 %copy-start.5 = (s32[1,256]{1,0:T(1,128)S(1)}, s32[1,256]{1,0:T(1,128)}, u32[]{:S(2)}) copy-start(s32[1,256]{1,0:T(1,128)} %get-tuple-element.8) | copy-start | bytes 3076
  282.5 563.9 %copy-start = (bf16[256,2048]{1,0:T(8,128)(2,1)S(1)}, bf16[256,2048]{1,0:T(8,128)(2,1)}, u32[]{:S(2)}) copy-start(bf16[256,2048]{1,0:T(8,128)(2,1)} %x_ref.3) | copy-start | bytes 3145732
  282.5 563.9 %copy-start.1 = (s32[256,8]{1,0:T(8,128)S(1)}, s32[256,8]{1,0:T(8,128)}, u32[]{:S(2)}) copy-start(s32[256,8]{1,0:T(8,128)} %copy.9.ids_ref) | copy-start | bytes 24580
  282.5 563.9 %copy-start.2 = (s32[256,8]{1,0:T(8,128)S(1)}, s32[256,8]{1,0:T(8,128)}, u32[]{:S(2)}) copy-start(s32[256,8]{1,0:T(8,128)} %get-tuple-element.7.slot_ref) | copy-start | bytes 24580
  282.5 563.9 %all-to-all-start.1 = ((bf16[128,32,2048]{2,1,0:T(8,128)(2,1)}), bf16[128,32,2048]{2,1,0:T(8,128)(2,1)}, u32[]{:S(2)}, u32[]{:S(2)}) async-start(bf16[128,32,2048]{2,1,0:T(8,128)(2,1)} %bitcast.12), calls=%async_computation.1 | async-start | bytes 33554432 | tf_op jit(solution)/shard_map/all_to_all | solution.py:152

commit v2 on v0

v2 whole, which is shorter than its diff:
```python
import functools

import jax
import jax.numpy as jnp
from jax import lax
from jax.experimental import pallas as pl
from jax.experimental.pallas import tpu as pltpu
from jax.sharding import PartitionSpec as P

MESH = pl.DeviceIdType.MESH
LANES = 16
RING = 4
STRIDE = {'x': 1, 'y': RING, 'z': RING * RING}
ORDERS = ('xyz', 'yzx', 'zxy')
WIDTHS = (640, 640, 768)
STARTS = (0, 640, 1280)
PARTS = range(3)


def place():
    chip = lax.axis_index('ep')
    coord = {axis: lax.rem(chip // stride, RING) for axis, stride in STRIDE.items()}
    return lax.axis_index('ep2'), chip, coord


class Item:
    def __init__(self, axis, source, target, half, dtype, switch=False):
        self.axis, self.source, self.target, self.half, self.dtype, self.switch = axis, source, target, half, dtype, switch


def exchange_kernel(items, partner, n_in, n_out, *refs):
    refs, scratch = refs[:n_in + n_out], refs[n_in + n_out:]
    relays, (send, recv, local) = scratch[:len(items)], scratch[len(items):]
    core, chip, coord = place()
    other = 1 - core
    axes = sorted({item.axis for item in items})
    switch = any(item.switch for item in items)

    def at(axis, step):
        pos = lax.rem(coord[axis] + step + RING, RING)
        return pos, chip + (pos - coord[axis]) * STRIDE[axis]

    barrier = pltpu.get_barrier_semaphore()
    peers = 0
    for axis in axes:
        for step in (1, -1):
            for c in ((core, other) if switch else (core,)):
                pl.semaphore_signal(barrier, inc=1, device_id=(0, c, at(axis, step)[1]), device_id_type=MESH)
                peers += 1
    if switch or partner:
        pl.semaphore_signal(barrier, inc=1, device_id=(0, other, chip), device_id_type=MESH)
        peers += 1
    pl.semaphore_wait(barrier, peers)

    def remote(i, src, dst, s, r, c, to):
        return pltpu.make_async_remote_copy(src_ref=src, dst_ref=dst, send_sem=send.at[i, s], recv_sem=recv.at[i, r], device_id=(0, c, to), device_id_type=MESH)

    sent, landed, kept = [], [], []
    for i, item in enumerate(items):
        far = at(item.axis, 2)[0]
        for h, step in ((0, 1), (1, -1)):
            copy = remote(i, item.source(refs, far, h), relays[i].at[h], h, h, core, at(item.axis, step)[1])
            copy.start()
            sent.append(copy)
    for i, item in enumerate(items):
        me = coord[item.axis]
        for d, step in ((0, 1), (1, -1)):
            pos, to = at(item.axis, step)
            for h in (0, 1):
                k, c = (core, h) if item.switch else (h, core)
                copy = remote(i, item.source(refs, pos, h), item.target(refs, me, k), 2 + 2 * d + h, 2 + 2 * d + k, c, to)
                copy.start()
                sent.append(copy)
    for i, item in enumerate(items):
        me = coord[item.axis]
        if item.switch:
            copy = remote(i, item.source(refs, me, other), item.target(refs, me, core), 8, 8, other, chip)
            copy.start()
            sent.append(copy)
            own = [(item.source(refs, me, core), item.target(refs, me, core))]
        else:
            own = [(item.source(refs, me, h), item.target(refs, me, h)) for h in (0, 1)]
        for h, (src, dst) in enumerate(own):
            copy = pltpu.make_async_copy(src, dst, local.at[i, h])
            copy.start()
            kept.append(copy)
    if partner:
        n = len(items)
        copy = remote(n, refs[partner[0]], refs[partner[1]], 0, 0, other, chip)
        copy.start()
        sent.append(copy)
    for i, item in enumerate(items):
        me = coord[item.axis]
        for h, step in ((0, 1), (1, -1)):
            remote(i, relays[i].at[h], relays[i].at[h], h, h, core, chip).wait_recv()
            to = at(item.axis, step)[1]
            k, c, r = (core, h, 6 + core) if item.switch else (h, core, 6 + h)
            copy = remote(i, relays[i].at[h], item.target(refs, at(item.axis, -step)[0], k), 6 + h, r, c, to)
            copy.start()
            sent.append(copy)
    for i, item in enumerate(items):
        me = coord[item.axis]
        for d, step in ((0, -1), (1, 1)):
            for k in (0, 1):
                dst = item.target(refs, at(item.axis, step)[0], k)
                remote(i, dst, dst, 2 + 2 * d + k, 2 + 2 * d + k, core, chip).wait_recv()
        for k in (0, 1):
            dst = item.target(refs, at(item.axis, 2)[0], k)
            remote(i, dst, dst, 6 + k, 6 + k, core, chip).wait_recv()
        if item.switch:
            dst = item.target(refs, me, other)
            remote(i, dst, dst, 8, 8, core, chip).wait_recv()
    if partner:
        dst = refs[partner[1]]
        remote(len(items), dst, dst, 0, 0, core, chip).wait_recv()
    for copy in kept:
        copy.wait()
    for copy in sent:
        copy.wait_send()


def exchange(name, collective_id, items, inputs, outputs, partner=None):
    anywhere = pl.BlockSpec(memory_space=pl.ANY)
    n = len(items)
    return pl.pallas_call(
        functools.partial(exchange_kernel, items, partner, len(inputs), len(outputs)),
        in_specs=[anywhere] * len(inputs),
        out_specs=[anywhere] * len(outputs),
        out_shape=[jax.ShapeDtypeStruct(shape, dtype) for shape, dtype in outputs],
        scratch_shapes=[pltpu.VMEM((2,) + item.half, item.dtype) for item in items]
        + [pltpu.SemaphoreType.DMA((n + 1, 9)), pltpu.SemaphoreType.DMA((n + 1, 9)), pltpu.SemaphoreType.DMA((n, 2))],
        compiler_params=pltpu.CompilerParams(collective_id=collective_id, has_side_effects=True),
        name=name,
    )(*inputs)


def route_kernel(ids_ref, slot_ref, count_ref):
    ids = ids_ref[...]
    n_top, n_tok = ids.shape
    experts = 2 * count_ref.shape[2]
    expert_of = lax.broadcasted_iota(jnp.int32, (experts, n_tok), 0)
    member = jnp.zeros((experts, n_tok), jnp.float32)
    for j in range(n_top):
        member = jnp.where(expert_of == ids[j:j + 1], 1.0, member)
    row = lax.broadcasted_iota(jnp.int32, (n_tok, n_tok), 0)
    col = lax.broadcasted_iota(jnp.int32, (n_tok, n_tok), 1)
    earlier = jnp.where(row < col, 1.0, 0.0).astype(jnp.bfloat16)
    member_lp = member.astype(jnp.bfloat16)
    before = jnp.dot(member_lp, earlier, preferred_element_type=jnp.float32)
    ones = jnp.ones((n_top, n_tok), jnp.bfloat16)
    counts = lax.dot_general(ones, member_lp, (((1,), (1,)), ((), ())), preferred_element_type=jnp.float32).astype(jnp.int32)
    half = n_tok // 2
    for h in (0, 1):
        count_ref[h] = counts[:, h * half:(h + 1) * half]
    for j in range(n_top):
        rank = jnp.sum(jnp.where(expert_of == ids[j:j + 1], before, 0.0), axis=0, keepdims=True)
        slot = ids[j:j + 1] * LANES + rank.astype(jnp.int32)
        for h in (0, 1):
            slot_ref[h, j:j + 1, :] = slot[:, h * half:(h + 1) * half]


def plane_slots(shape, order, coord):
    row = lax.broadcasted_iota(jnp.int32, shape, 0)
    per_dev = 2 * LANES
    third = (row >> 5) & (RING - 1)
    core = (row >> 7) & 1
    second = row >> 8
    first, stride = coord[order[0]], [STRIDE[axis] for axis in order]
    dev = core * RING**3 + second * stride[1] + third * stride[2] + first * stride[0]
    return dev * per_dev + (row & (per_dev - 1))


def pack_kernel(*refs):
    slots, tokens, outs = refs[:3], refs[3:6], refs[6:]
    _, _, coord = place()
    for r in PARTS:
        n_tok = tokens[r].shape[1]
        rows = 2 * RING * RING * 2 * LANES
        wanted = plane_slots((rows, n_tok // 2), ORDERS[r], coord)
        picks = []
        for h in (0, 1):
            pick = jnp.zeros((rows, n_tok // 2), jnp.float32)
            for j in range(slots[r].shape[2]):
                pick = jnp.where(wanted == slots[r][0, h, j:j + 1], 1.0, pick)
            picks.append(pick.astype(jnp.bfloat16))
        got = jnp.dot(jnp.concatenate(picks, axis=1), tokens[r][0], preferred_element_type=jnp.float32).astype(jnp.bfloat16)
        outs[r][...] = got.reshape(outs[r].shape)


def pack(slots, tokens):
    lead = (RING, 2, RING)
    return pl.pallas_call(
        pack_kernel,
        grid=(RING,),
        in_specs=[pl.BlockSpec((1,) + s.shape[1:], lambda a: (a, 0, 0, 0)) for s in slots]
        + [pl.BlockSpec((1,) + t.shape[1:], lambda a: (a, 0, 0)) for t in tokens],
        out_specs=[pl.BlockSpec(lead + (1, 2 * LANES, w), lambda a: (0, 0, 0, a, 0, 0)) for w in WIDTHS],
        out_shape=[jax.ShapeDtypeStruct(lead + (RING, 2 * LANES, w), jnp.bfloat16) for w in WIDTHS],
        compiler_params=pltpu.CompilerParams(vmem_limit_bytes=48 * 2**20),
        name='pack',
    )(*slots, *tokens)


def expert_kernel(*refs):
    ins, (w_in_ref, w_out_ref), outs = refs[:3], refs[3:5], refs[5:]
    total = None
    for r in PARTS:
        shape = ins[r].shape
        rows = ins[r][...].reshape(shape[0] * shape[2], shape[3])
        term = jnp.dot(rows, w_in_ref[0, STARTS[r]:STARTS[r] + WIDTHS[r]], preferred_element_type=jnp.float32)
        total = term if total is None else total + term
    hidden = jax.nn.gelu(total, approximate=True).astype(jnp.bfloat16)
    for r in PARTS:
        out = jnp.dot(hidden, w_out_ref[0, :, STARTS[r]:STARTS[r] + WIDTHS[r]], preferred_element_type=jnp.float32)
        outs[r][...] = out.astype(jnp.bfloat16).reshape(outs[r].shape)


def expert(parts, w_in, w_out, group=32):
    e_loc, d_model, ff = w_in.shape
    shape = (2 * RING**3, e_loc, LANES)
    specs = [pl.BlockSpec((group, 1, LANES, w), lambda e, i: (i, e, 0, 0)) for w in WIDTHS]
    return pl.pallas_call(
        expert_kernel,
        grid=(e_loc, shape[0] // group),
        in_specs=specs + [pl.BlockSpec((1, d_model, ff), lambda e, i: (e, 0, 0)), pl.BlockSpec((1, ff, d_model), lambda e, i: (e, 0, 0))],
        out_specs=specs,
        out_shape=[jax.ShapeDtypeStruct(shape + (w,), jnp.bfloat16) for w in WIDTHS],
        compiler_params=pltpu.CompilerParams(vmem_limit_bytes=48 * 2**20),
        name='expert',
    )(*[p.reshape(shape + (w,)) for p, w in zip(parts, WIDTHS)], w_in, w_out)


def weight_kernel(capacity, ids_ref, slot_ref, gate_ref, mine_ref, partner_ref, out_ref):
    core, chip, _ = place()
    ids, gate = ids_ref[...], gate_ref[...]
    n_top, n_tok = ids.shape
    mine = mine_ref[...]
    ahead = lax.broadcasted_iota(jnp.int32, mine.shape, 0) < chip
    off = jnp.sum(jnp.where(ahead, mine, 0), axis=0) + jnp.where(core == 1, jnp.sum(partner_ref[...], axis=0), 0)
    off = jnp.concatenate([off[0], off[1]], axis=1)
    high = (off >> 7).astype(jnp.bfloat16)
    low = (off & 127).astype(jnp.bfloat16)
    expert_of = lax.broadcasted_iota(jnp.int32, (off.shape[1], n_tok), 0)
    half = n_tok // 2
    for j in range(n_top):
        choice = jnp.where(expert_of == ids[j:j + 1], 1.0, 0.0).astype(jnp.bfloat16)
        first = 128 * jnp.dot(high, choice, preferred_element_type=jnp.float32) + jnp.dot(low, choice, preferred_element_type=jnp.float32)
        first = first[0:1].astype(jnp.int32)
        for h in (0, 1):
            cut = slice(h * half, (h + 1) * half)
            rank = first[:, cut] + slot_ref[h, j:j + 1] - ids[j:j + 1, cut] * LANES
            out_ref[h, j:j + 1] = jnp.where(rank < capacity, gate[j:j + 1, cut], 0.0)


def combine_kernel(*refs):
    slots, gates, backs, outs = refs[:3], refs[3:6], refs[6:9], refs[9:]
    _, _, coord = place()
    for r in PARTS:
        n_tok = outs[r].shape[1]
        rows = 2 * RING * RING * 2 * LANES
        wanted = plane_slots((rows, n_tok // 2), ORDERS[r], coord)
        back = backs[r][...].reshape(rows, WIDTHS[r])
        for h in (0, 1):
            gate = jnp.zeros((rows, n_tok // 2), jnp.float32)
            for j in range(slots[r].shape[2]):
                gate = jnp.where(wanted == slots[r][0, h, j:j + 1], gates[r][0, h, j:j + 1], gate)
            high = gate.astype(jnp.bfloat16)
            rest = gate - high.astype(jnp.float32)
            mid = rest.astype(jnp.bfloat16)
            low = (rest - mid.astype(jnp.float32)).astype(jnp.bfloat16)
            gate3 = jnp.concatenate([high, mid, low], axis=1)
            mix = lax.dot_general(gate3, back, (((0,), (0,)), ((), ())), preferred_element_type=jnp.float32)
            n = n_tok // 2
            outs[r][0, h * n:(h + 1) * n] = mix[:n] + mix[n:2 * n] + mix[2 * n:]


def combine(slots, gates, backs, n_tok):
    lead = (RING, 2, RING)
    small = [pl.BlockSpec((1,) + s.shape[1:], lambda a: (a, 0, 0, 0)) for s in slots]
    return pl.pallas_call(
        combine_kernel,
        grid=(RING,),
        in_specs=small + small + [pl.BlockSpec(lead + (1, 2 * LANES, w), lambda a: (0, 0, 0, a, 0, 0)) for w in WIDTHS],
        out_specs=[pl.BlockSpec((1, n_tok, w), lambda a: (a, 0, 0)) for w in WIDTHS],
        out_shape=[jax.ShapeDtypeStruct((RING, n_tok, w), jnp.float32) for w in WIDTHS],
        compiler_params=pltpu.CompilerParams(vmem_limit_bytes=48 * 2**20),
        name='combine',
    )(*slots, *gates, *backs)


def final_kernel(x_ref, *refs):
    parts, out_ref = refs[:3], refs[3]
    for r in PARTS:
        cut = slice(STARTS[r], STARTS[r] + WIDTHS[r])
        total = x_ref[:, cut].astype(jnp.float32)
        for a in range(RING):
            total += parts[r][a]
        out_ref[:, cut] = total.astype(out_ref.dtype)


def final(x, parts, rows=64):
    n_tok, d_model = x.shape
    return pl.pallas_call(
        final_kernel,
        grid=(n_tok // rows,),
        in_specs=[pl.BlockSpec((rows, d_model), lambda i: (i, 0))] + [pl.BlockSpec((RING, rows, w), lambda i: (0, i, 0)) for w in WIDTHS],
        out_specs=pl.BlockSpec((rows, d_model), lambda i: (i, 0)),
        out_shape=jax.ShapeDtypeStruct(x.shape, x.dtype),
        name='final',
    )(x, *parts)


def spot(axis, order, index):
    return (slice(None),) * [a for a in 'zyx' if a in order].index(axis) + (index,)


def solution(mesh):
    dev_axes = ('ep2', 'ep')
    bf16, f32, i32 = jnp.bfloat16, jnp.float32, jnp.int32
    group_size = mesh.shape['ep2'] * mesh.shape['ep']

    def local_step(x, ids, gate, w_a, w_b):
        n_tok, d_model = x.shape
        n_top = ids.shape[1]
        experts = w_a.shape[0] * group_size
        capacity = 8 * ((5 * group_size * n_tok * n_top) // (32 * experts))
        small = (2, n_top, n_tok // 2)
        ids_t, gate_t = ids.T, gate.T
        slot, counts = pl.pallas_call(route_kernel, out_shape=(jax.ShapeDtypeStruct(small, i32), jax.ShapeDtypeStruct((2, n_top, experts // 2), i32)), name='route')(ids_t)
        tile = (n_top, n_tok // 2)
        half_tok = n_tok // 2
        block = (RING, RING, 2 * LANES)
        first = [o[0] for o in ORDERS]
        second = [o[1] for o in ORDERS]
        third = [o[2] for o in ORDERS]

        items = [Item(first[r], lambda f, p, h, r=r: f[0].at[pl.ds(h * half_tok, half_tok), pl.ds(STARTS[r], WIDTHS[r])],
                      lambda f, o, k, r=r: f[3 + r].at[o, pl.ds(k * half_tok, half_tok)], (half_tok, WIDTHS[r]), bf16) for r in PARTS]
        items += [Item(first[r], lambda f, p, h: f[1].at[h], lambda f, o, k, r=r: f[6 + r].at[o, k], tile, i32) for r in PARTS]
        items += [Item('x', lambda f, p, h: f[2].at[h], lambda f, o, k: f[9].at[o, k], tile, i32)]
        outs = exchange('stage_a', 0, items, [x, slot, counts],
                        [((RING, n_tok, w), bf16) for w in WIDTHS] + [((RING,) + small, i32)] * 4)
        tokens, slots, count_x = outs[:3], outs[3:6], outs[6]
        sends = pack(slots, tokens)

        items = [Item(second[r], lambda f, p, h, r=r: f[r].at[p, h],
                      lambda f, o, k, r=r: f[4 + r].at[(slice(None), k) + spot(second[r], ORDERS[r][:2], o)], block + (WIDTHS[r],), bf16, True) for r in PARTS]
        items += [Item('y', lambda f, p, h: f[3].at[:, h], lambda f, o, k: f[7].at[o, :, k], (RING,) + tile, i32)]
        mids = exchange('stage_b', 1, items, [*sends, count_x],
                        [((RING, 2) + block + (w,), bf16) for w in WIDTHS] + [((RING, RING) + small, i32)])

        items = [Item(third[r], lambda f, p, h, r=r: f[r].at[p, h],
                      lambda f, o, k, r=r: f[4 + r].at[(k,) + spot(third[r], 'zyx', o)], block + (WIDTHS[r],), bf16) for r in PARTS]
        items += [Item('z', lambda f, p, h: f[3].at[:, :, h], lambda f, o, k: f[7].at[o, :, :, k], (RING, RING) + tile, i32)]
        outs = exchange('stage_c', 2, items, list(mids),
                        [((2, RING) + block + (w,), bf16) for w in WIDTHS] + [((RING, RING, RING) + small, i32)])
        count_z = outs[3]
        results = expert(outs[:3], w_a, w_b)
        results = [o.reshape((2, RING) + block + (w,)) for o, w in zip(results, WIDTHS)]

        items = [Item(third[r], lambda f, p, h, r=r: f[r].at[(h,) + spot(third[r], 'zyx', p)],
                      lambda f, o, k, r=r: f[4 + r].at[o, k], block + (WIDTHS[r],), bf16) for r in PARTS]
        outs = exchange('stage_c_back', 3, items, [*results, count_z],
                        [((RING, 2) + block + (w,), bf16) for w in WIDTHS] + [(count_z.shape, i32)], partner=(3, 7))
        mids, count_other = outs[:3], outs[3]
        chips = (RING**3,) + small
        gates = pl.pallas_call(functools.partial(weight_kernel, capacity), out_shape=jax.ShapeDtypeStruct(small, f32), name='weight')(
            ids_t, slot, gate_t, count_z.reshape(chips), count_other.reshape(chips))
        items = [Item(second[r], lambda f, p, h, r=r: f[r].at[(slice(None), h) + spot(second[r], ORDERS[r][:2], p)],
                      lambda f, o, k, r=r: f[4 + r].at[o, k], block + (WIDTHS[r],), bf16, True) for r in PARTS]
        items += [Item(first[r], lambda f, p, h: f[3].at[h], lambda f, o, k, r=r: f[7 + r].at[o, k], tile, f32) for r in PARTS]
        outs = exchange('stage_b_back', 4, items, [*mids, gates],
                        [((RING, 2) + block + (w,), bf16) for w in WIDTHS] + [((RING,) + small, f32)] * 3)
        partial = combine(slots, outs[3:], outs[:3], n_tok)

        items = [Item(first[r], lambda f, p, h, r=r: f[r].at[p, pl.ds(h * half_tok, half_tok)],
                      lambda f, o, k, r=r: f[3 + r].at[o, pl.ds(k * half_tok, half_tok)], (half_tok, WIDTHS[r]), f32) for r in PARTS]
        parts = exchange('stage_a_back', 5, items, list(partial), [((RING, n_tok, w), f32) for w in WIDTHS])
        return final(x, parts)

    tok_spec = P(('dp', 'ep2', 'ep'), None)
    w_spec = P(dev_axes, None, None)
    return jax.shard_map(local_step, mesh=mesh, in_specs=(tok_spec, tok_spec, tok_spec, w_spec, w_spec), out_specs=tok_spec, check_vma=False)
```

time: 901 us -> 606 us (0.67)
  the two profiles are of different devices: /device:TPU:8 before, /device:TPU:1 now
where the time goes in v2:
time: 606 us
  Pallas kernels  592 us (98%)
  local copies, waits for them, and re-layouts  13.8 us (2%)
    pallas_call x6, Pallas kernels, exchange(): pl.pallas_call(functools.partial(exchange_kernel, items, partner, len(inp...  520 us
    pallas_call x1, Pallas kernels, expert(): pl.pallas_call(expert_kernel, grid=(e_loc, shape[0] // group), in_specs=s...  26.6 us
    pallas_call x1, Pallas kernels, combine(): pl.pallas_call(combine_kernel, grid=(RING,), in_specs=small + small + [pl...  21.7 us
    pallas_call x1, Pallas kernels, pack(): pl.pallas_call(pack_kernel, grid=(RING,), in_specs=[pl.BlockSpec((1,) + s...  13.9 us
    unnamed x30, local copies, waits for them, and re-layouts  13.8 us

profile of v2, /device:TPU:1, one launch (start us, length us, event | category | flops | bytes accessed | tf_op | source)
XLA Modules:
  0.0 605.7 jit_solution(6229375829388945833)
XLA Ops:
  0.0 1.8 route.1
  1.8 40.2 %stage_a.1 = (bf16[4,256,640]{2,1,0:T(8,128)(2,1)}, bf16[4,256,640]{2,1,0:T(8,128)(2,1)}, bf16[4,256,768]{2,1,0:T(8,128)(2,1)}, s32[4,2,8,128]{3,2,1,0:T(8,128)}...) custom-call(bf16[256,2048]{1,0:T(8,128)(2,1)} %x_ref.1, ...), custom_call_target="tpu_custom_call" | custom-call | tf_op jit(solution)/shard_map/stage_a/pallas_call | solution.py:125
  42.0 1.4 copy-done.3
  43.4 1.3 copy-done.4
  44.7 1.3 copy-done.5
  46.1 0.8 copy-done.6
  46.8 0.8 copy-done.8
  47.6 0.8 copy-done.10
  48.3 13.9 %pack.1 = (bf16[4,2,4,4,32,640]{5,4,3,2,1,0:T(8,128)(2,1)}, bf16[4,2,4,4,32,640]{5,4,3,2,1,0:T(8,128)(2,1)}, bf16[4,2,4,4,32,768]{5,4,3,2,1,0:T(8,128)(2,1)}) custom-call(s32[4,2,8,128]{3,2,1,0:T(8,128)S(1)} %copy-done.6, s32[4,2,8,128]{3,2,1,0:T(8,128)S(1)} %copy-done.8, s32[4,2,8,128]{3,2,1,0:T(8,128)S(1)} %copy-done.10, ...), custom_call_target="tpu_custom_call" | custom-call | tf_op jit(solution)/shard_map/pack/pallas_call | solution.py:192
  62.2 74.5 %stage_b.1 = (bf16[4,2,4,4,32,640]{5,4,3,2,1,0:T(8,128)(2,1)}, bf16[4,2,4,4,32,640]{5,4,3,2,1,0:T(8,128)(2,1)}, bf16[4,2,4,4,32,768]{5,4,3,2,1,0:T(8,128)(2,1)}, s32[4,4,2,8,128]{4,3,2,1,0:T(8,128)}) custom-call(bf16[4,2,4,4,32,640]{5,4,3,2,1,0:T(8,128)(2,1)} %get-tuple-element.52.refs_0_, bf16[4,2,4,4,32,640]{5,4,3,2,1,0:T(8,128)(2,1)} %get-tuple-element.53.refs_1_, ...), custom_call_target="tpu_custom_call" | custom-call | tf_op jit(solution)/shard_map/stage_b/pallas_call | solution.py:125
  136.8 134.5 %stage_c.1 = (bf16[2,4,4,4,32,640]{5,4,3,2,1,0:T(8,128)(2,1)}, bf16[2,4,4,4,32,640]{5,4,3,2,1,0:T(8,128)(2,1)}, bf16[2,4,4,4,32,768]{5,4,3,2,1,0:T(8,128)(2,1)}, s32[4,4,4,2,8,128]{5,4,3,2,1,0:T(8,128)}) custom-call(bf16[4,2,4,4,32,640]{5,4,3,2,1,0:T(8,128)(2,1)} %get-tuple-element.56.refs_0_, bf16[4,2,4,4,32,640]{5,4,3,2,1,0:T(8,128)(2,1)} %get-tuple-element.57.refs_1_, ...), custom_call_target="tpu_custom_call" | custom-call | tf_op jit(solution)/shard_map/stage_c/pallas_call | solution.py:125
  271.2 2.2 copy-done
  273.4 26.6 %expert.1 = (bf16[128,2,16,640]{3,2,1,0:T(8,128)(2,1)}, bf16[128,2,16,640]{3,2,1,0:T(8,128)(2,1)}, bf16[128,2,16,768]{3,2,1,0:T(8,128)(2,1)}) custom-call(bf16[128,2,16,640]{3,2,1,0:T(8,128)(2,1)} %bitcast.14, bf16[128,2,16,640]{3,2,1,0:T(8,128)(2,1)} %bitcast.15, bf16[128,2,16,768]{3,2,1,0:T(8,128)(2,1)} %bitcast.11, bf16[2,2048,512]{2,1,0:T(8,128)(2,1)S(1)} %copy-done, ...), custom_call_target="tpu_custom_call" | custom-call | tf_op jit(solution)/shard_map/expert/pallas_call | solution.py:222
  300.0 131.2 %stage_c_back.1 = (bf16[4,2,4,4,32,640]{5,4,3,2,1,0:T(8,128)(2,1)}, bf16[4,2,4,4,32,640]{5,4,3,2,1,0:T(8,128)(2,1)}, bf16[4,2,4,4,32,768]{5,4,3,2,1,0:T(8,128)(2,1)}, s32[4,4,4,2,8,128]{5,4,3,2,1,0:T(8,128)}) custom-call(bf16[2,4,4,4,32,640]{5,4,3,2,1,0:T(8,128)(2,1)} %bitcast.12, bf16[2,4,4,4,32,640]{5,4,3,2,1,0:T(8,128)(2,1)} %bitcast.13, ...), custom_call_target="tpu_custom_call" | custom-call | tf_op jit(solution)/shard_map/stage_c_back/pallas_call | solution.py:125
  431.2 2.3 weight.1.refs_3_
  433.6 73.9 %stage_b_back.1 = (bf16[4,2,4,4,32,640]{5,4,3,2,1,0:T(8,128)(2,1)}, bf16[4,2,4,4,32,640]{5,4,3,2,1,0:T(8,128)(2,1)}, bf16[4,2,4,4,32,768]{5,4,3,2,1,0:T(8,128)(2...) custom-call(bf16[4,2,4,4,32,640]{5,4,3,2,1,0:T(8,128)(2,1)} %get-tuple-element.67.refs_0_, ...), custom_call_target="tpu_custom_call" | custom-call | tf_op jit(solution)/shard_map/stage_b_back/pallas_call | solution.py:125
  507.5 0.7 copy-done.12
  508.3 0.8 copy-done.13
  509.0 0.8 copy-done.14
  509.8 21.7 %combine.1 = (f32[4,256,640]{2,1,0:T(8,128)S(1)}, f32[4,256,640]{2,1,0:T(8,128)S(1)}, f32[4,256,768]{2,1,0:T(8,128)}) custom-call(s32[4,2,8,128]{3,2,1,0:T(8,128)S(1)} %copy-done.7, s32[4,2,8,128]{3,2,1,0:T(8,128)S(1)} %copy-done.9, s32[4,2,8,128]{3,2,1,0:T(8,128)S(1)} %copy-done.11, f32[4,2,8,128]{3,2,1,0:T(8,128)S(1)} %copy-done.12, ...), custom_call_target="tpu_custom_call" | custom-call | tf_op jit(solution)/shard_map/combine/pallas_call | solution.py:280
  531.5 1.5 copy-done.1
  533.0 1.5 copy-done.2
  534.5 66.1 %stage_a_back.1 = (f32[4,256,640]{2,1,0:T(8,128)}, f32[4,256,640]{2,1,0:T(8,128)}, f32[4,256,768]{2,1,0:T(8,128)}) custom-call(f32[4,256,640]{2,1,0:T(8,128)} %copy-done.1, f32[4,256,640]{2,1,0:T(8,128)} %copy-done.2, f32[4,256,768]{2,1,0:T(8,128)} %get-tuple-element.79.refs_2_), custom_call_target="tpu_custom_call" | custom-call | tf_op jit(solution)/shard_map/stage_a_back/pallas_call | solution.py:125
  600.6 5.2 final.1
  (18 shorter events, 0.0 us)
Async XLA Ops:
  42.0 1.4 copy-start.3
  43.4 1.3 copy-start.4
  44.7 1.3 copy-start.5
  46.1 0.8 copy-start.6
  46.8 0.8 copy-start.8
  47.6 0.8 copy-start.10
  271.2 2.2 copy-start
  433.6 73.9 %copy-start.7 = (s32[4,2,8,128]{3,2,1,0:T(8,128)S(1)}, s32[4,2,8,128]{3,2,1,0:T(8,128)}, u32[]{:S(2)}) copy-start(s32[4,2,8,128]{3,2,1,0:T(8,128)} %get-tuple-element.46.refs_0_) | copy-start | bytes 98308
  433.6 73.9 %copy-start.9 = (s32[4,2,8,128]{3,2,1,0:T(8,128)S(1)}, s32[4,2,8,128]{3,2,1,0:T(8,128)}, u32[]{:S(2)}) copy-start(s32[4,2,8,128]{3,2,1,0:T(8,128)} %get-tuple-element.47.refs_1_) | copy-start | bytes 98308
  433.6 73.9 %copy-start.11 = (s32[4,2,8,128]{3,2,1,0:T(8,128)S(1)}, s32[4,2,8,128]{3,2,1,0:T(8,128)}, u32[]{:S(2)}) copy-start(s32[4,2,8,128]{3,2,1,0:T(8,128)} %get-tuple-element.48.refs_2_) | copy-start | bytes 98308
  507.5 0.8 copy-start.12
  508.3 0.8 copy-start.13
  509.0 0.8 copy-start.14
  531.5 1.5 copy-start.1
  533.0 1.5 copy-start.2

commit v3 on v2

--- a/solution.py
+++ b/solution.py
@@ -30,9 +30,17 @@
 
 def exchange_kernel(items, partner, n_in, n_out, *refs):
     refs, scratch = refs[:n_in + n_out], refs[n_in + n_out:]
-    relays, (send, recv, local) = scratch[:len(items)], scratch[len(items):]
+    relays, bounces, (send, recv, local) = scratch[:len(items)], scratch[len(items):2 * len(items)], scratch[2 * len(items):]
     core, chip, coord = place()
     other = 1 - core
+    loads = []
+    for i, item in enumerate(items):
+        me = coord[item.axis]
+        own = [(core, core)] if item.switch else [(0, 0), (1, 1)]
+        for n, (h, k) in enumerate(own):
+            copy = pltpu.make_async_copy(item.source(refs, me, h), bounces[i].at[n], local.at[i, n])
+            copy.start()
+            loads.append((copy, bounces[i].at[n], item.target(refs, me, k), local.at[i, 2 + n]))
     axes = sorted({item.axis for item in items})
     switch = any(item.switch for item in items)
 
@@ -77,20 +85,17 @@
             copy = remote(i, item.source(refs, me, other), item.target(refs, me, core), 8, 8, other, chip)
             copy.start()
             sent.append(copy)
-            own = [(item.source(refs, me, core), item.target(refs, me, core))]
-        else:
-            own = [(item.source(refs, me, h), item.target(refs, me, h)) for h in (0, 1)]
-        for h, (src, dst) in enumerate(own):
-            copy = pltpu.make_async_copy(src, dst, local.at[i, h])
-            copy.start()
-            kept.append(copy)
     if partner:
         n = len(items)
         copy = remote(n, refs[partner[0]], refs[partner[1]], 0, 0, other, chip)
         copy.start()
         sent.append(copy)
-    for i, item in enumerate(items):
-        me = coord[item.axis]
+    for load, src, dst, sem in loads:
+        load.wait()
+        copy = pltpu.make_async_copy(src, dst, sem)
+        copy.start()
+        kept.append(copy)
+    for i, item in enumerate(items):
         for h, step in ((0, 1), (1, -1)):
             remote(i, relays[i].at[h], relays[i].at[h], h, h, core, chip).wait_recv()
             to = at(item.axis, step)[1]
@@ -128,7 +133,8 @@
         out_specs=[anywhere] * len(outputs),
         out_shape=[jax.ShapeDtypeStruct(shape, dtype) for shape, dtype in outputs],
         scratch_shapes=[pltpu.VMEM((2,) + item.half, item.dtype) for item in items]
-        + [pltpu.SemaphoreType.DMA((n + 1, 9)), pltpu.SemaphoreType.DMA((n + 1, 9)), pltpu.SemaphoreType.DMA((n, 2))],
+        + [pltpu.VMEM((1 if item.switch else 2,) + item.half, item.dtype) for item in items]
+        + [pltpu.SemaphoreType.DMA((n + 1, 9)), pltpu.SemaphoreType.DMA((n + 1, 9)), pltpu.SemaphoreType.DMA((n, 4))],
         compiler_params=pltpu.CompilerParams(collective_id=collective_id, has_side_effects=True),
         name=name,
     )(*inputs)

time: 606 us -> 442 us (0.73)
  Pallas kernels: 592 us -> 427 us
    pallas_call x6, Pallas kernels: 520 us -> 355 us  [exchange(): pl.pallas_call(functools.partial(exchange_kernel, items, partner, len(inp...]
where the time goes in v3:
time: 442 us; the launch traced here: 441 us
  Pallas kernels  427 us (97%)
  local copies, waits for them, and re-layouts  13.8 us (3%)
    pallas_call x6, Pallas kernels, exchange(): pl.pallas_call(functools.partial(exchange_kernel, items, partner, len(inp...  355 us
    pallas_call x1, Pallas kernels, expert(): pl.pallas_call(expert_kernel, grid=(e_loc, shape[0] // group), in_specs=s...  26.6 us
    pallas_call x1, Pallas kernels, combine(): pl.pallas_call(combine_kernel, grid=(RING,), in_specs=small + small + [pl...  21.7 us
    pallas_call x1, Pallas kernels, pack(): pl.pallas_call(pack_kernel, grid=(RING,), in_specs=[pl.BlockSpec((1,) + s...  13.9 us
    unnamed x30, local copies, waits for them, and re-layouts  13.8 us

profile of v3, /device:TPU:1, one launch (start us, length us, event | category | flops | bytes accessed | tf_op | source)
XLA Modules:
  0.0 440.7 jit_solution(11357635946324470182)
XLA Ops:
  0.0 1.8 route.1
  1.8 26.4 %stage_a.1 = (bf16[4,256,640]{2,1,0:T(8,128)(2,1)}, bf16[4,256,640]{2,1,0:T(8,128)(2,1)}, bf16[4,256,768]{2,1,0:T(8,128)(2,1)}, s32[4,2,8,128]{3,2,1,0:T(8,128)}...) custom-call(bf16[256,2048]{1,0:T(8,128)(2,1)} %x_ref.1, ...), custom_call_target="tpu_custom_call" | custom-call | tf_op jit(solution)/shard_map/stage_a/pallas_call | solution.py:130
  28.3 1.4 copy-done.3
  29.7 1.3 copy-done.4
  31.0 1.3 copy-done.5
  32.3 0.8 copy-done.6
  33.1 0.8 copy-done.8
  33.8 0.8 copy-done.10
  34.6 13.9 %pack.1 = (bf16[4,2,4,4,32,640]{5,4,3,2,1,0:T(8,128)(2,1)}, bf16[4,2,4,4,32,640]{5,4,3,2,1,0:T(8,128)(2,1)}, bf16[4,2,4,4,32,768]{5,4,3,2,1,0:T(8,128)(2,1)}) custom-call(s32[4,2,8,128]{3,2,1,0:T(8,128)S(1)} %copy-done.6, s32[4,2,8,128]{3,2,1,0:T(8,128)S(1)} %copy-done.8, s32[4,2,8,128]{3,2,1,0:T(8,128)S(1)} %copy-done.10, ...), custom_call_target="tpu_custom_call" | custom-call | tf_op jit(solution)/shard_map/pack/pallas_call | solution.py:198
  48.5 73.5 %stage_b.1 = (bf16[4,2,4,4,32,640]{5,4,3,2,1,0:T(8,128)(2,1)}, bf16[4,2,4,4,32,640]{5,4,3,2,1,0:T(8,128)(2,1)}, bf16[4,2,4,4,32,768]{5,4,3,2,1,0:T(8,128)(2,1)}, s32[4,4,2,8,128]{4,3,2,1,0:T(8,128)}) custom-call(bf16[4,2,4,4,32,640]{5,4,3,2,1,0:T(8,128)(2,1)} %get-tuple-element.52.refs_0_, bf16[4,2,4,4,32,640]{5,4,3,2,1,0:T(8,128)(2,1)} %get-tuple-element.53.refs_1_, ...), custom_call_target="tpu_custom_call" | custom-call | tf_op jit(solution)/shard_map/stage_b/pallas_call | solution.py:130
  122.0 71.5 %stage_c.1 = (bf16[2,4,4,4,32,640]{5,4,3,2,1,0:T(8,128)(2,1)}, bf16[2,4,4,4,32,640]{5,4,3,2,1,0:T(8,128)(2,1)}, bf16[2,4,4,4,32,768]{5,4,3,2,1,0:T(8,128)(2,1)}, s32[4,4,4,2,8,128]{5,4,3,2,1,0:T(8,128)}) custom-call(bf16[4,2,4,4,32,640]{5,4,3,2,1,0:T(8,128)(2,1)} %get-tuple-element.56.refs_0_, bf16[4,2,4,4,32,640]{5,4,3,2,1,0:T(8,128)(2,1)} %get-tuple-element.57.refs_1_, ...), custom_call_target="tpu_custom_call" | custom-call | tf_op jit(solution)/shard_map/stage_c/pallas_call | solution.py:130
  193.6 2.2 copy-done
  195.8 26.6 %expert.1 = (bf16[128,2,16,640]{3,2,1,0:T(8,128)(2,1)}, bf16[128,2,16,640]{3,2,1,0:T(8,128)(2,1)}, bf16[128,2,16,768]{3,2,1,0:T(8,128)(2,1)}) custom-call(bf16[128,2,16,640]{3,2,1,0:T(8,128)(2,1)} %bitcast.14, bf16[128,2,16,640]{3,2,1,0:T(8,128)(2,1)} %bitcast.15, bf16[128,2,16,768]{3,2,1,0:T(8,128)(2,1)} %bitcast.11, bf16[2,2048,512]{2,1,0:T(8,128)(2,1)S(1)} %copy-done, ...), custom_call_target="tpu_custom_call" | custom-call | tf_op jit(solution)/shard_map/expert/pallas_call | solution.py:228
  222.3 72.3 %stage_c_back.1 = (bf16[4,2,4,4,32,640]{5,4,3,2,1,0:T(8,128)(2,1)}, bf16[4,2,4,4,32,640]{5,4,3,2,1,0:T(8,128)(2,1)}, bf16[4,2,4,4,32,768]{5,4,3,2,1,0:T(8,128)(2,1)}, s32[4,4,4,2,8,128]{5,4,3,2,1,0:T(8,128)}) custom-call(bf16[2,4,4,4,32,640]{5,4,3,2,1,0:T(8,128)(2,1)} %bitcast.12, bf16[2,4,4,4,32,640]{5,4,3,2,1,0:T(8,128)(2,1)} %bitcast.13, ...), custom_call_target="tpu_custom_call" | custom-call | tf_op jit(solution)/shard_map/stage_c_back/pallas_call | solution.py:130
  294.7 2.3 weight.1.refs_3_
  297.0 74.1 %stage_b_back.1 = (bf16[4,2,4,4,32,640]{5,4,3,2,1,0:T(8,128)(2,1)}, bf16[4,2,4,4,32,640]{5,4,3,2,1,0:T(8,128)(2,1)}, bf16[4,2,4,4,32,768]{5,4,3,2,1,0:T(8,128)(2...) custom-call(bf16[4,2,4,4,32,640]{5,4,3,2,1,0:T(8,128)(2,1)} %get-tuple-element.67.refs_0_, ...), custom_call_target="tpu_custom_call" | custom-call | tf_op jit(solution)/shard_map/stage_b_back/pallas_call | solution.py:130
  371.1 0.7 copy-done.12
  371.9 0.8 copy-done.13
  372.6 0.8 copy-done.14
  373.4 21.7 %combine.1 = (f32[4,256,640]{2,1,0:T(8,128)S(1)}, f32[4,256,640]{2,1,0:T(8,128)S(1)}, f32[4,256,768]{2,1,0:T(8,128)}) custom-call(s32[4,2,8,128]{3,2,1,0:T(8,128)S(1)} %copy-done.7, s32[4,2,8,128]{3,2,1,0:T(8,128)S(1)} %copy-done.9, s32[4,2,8,128]{3,2,1,0:T(8,128)S(1)} %copy-done.11, f32[4,2,8,128]{3,2,1,0:T(8,128)S(1)} %copy-done.12, ...), custom_call_target="tpu_custom_call" | custom-call | tf_op jit(solution)/shard_map/combine/pallas_call | solution.py:286
  395.1 1.5 copy-done.1
  396.6 1.5 copy-done.2
  398.1 37.4 %stage_a_back.1 = (f32[4,256,640]{2,1,0:T(8,128)}, f32[4,256,640]{2,1,0:T(8,128)}, f32[4,256,768]{2,1,0:T(8,128)}) custom-call(f32[4,256,640]{2,1,0:T(8,128)} %copy-done.1, f32[4,256,640]{2,1,0:T(8,128)} %copy-done.2, f32[4,256,768]{2,1,0:T(8,128)} %get-tuple-element.79.refs_2_), custom_call_target="tpu_custom_call" | custom-call | tf_op jit(solution)/shard_map/stage_a_back/pallas_call | solution.py:130
  435.5 5.2 %final.1 = bf16[256,2048]{1,0:T(8,128)(2,1)} custom-call(bf16[256,2048]{1,0:T(8,128)(2,1)} %x_ref.1, f32[4,256,640]{2,1,0:T(8,128)} %get-tuple-element.80.refs_0_, f32[4,256,640]{2,1,0:T(8,128)} %get-tuple-element.81.refs_1_, f32[4,256,768]{2,1,0:T(8,128)} %get-tuple-element.82.refs_2_), custom_call_target="tpu_custom_call" | custom-call | tf_op jit(solution)/shard_map/final/pallas_call | solution.py:309
  (18 shorter events, 0.0 us)
Async XLA Ops:
  28.3 1.4 copy-start.3
  29.7 1.3 copy-start.4
  31.0 1.3 copy-start.5
  32.3 0.8 copy-start.6
  33.1 0.8 copy-start.8
  33.8 0.8 copy-start.10
  193.6 2.2 copy-start
  297.0 74.1 %copy-start.7 = (s32[4,2,8,128]{3,2,1,0:T(8,128)S(1)}, s32[4,2,8,128]{3,2,1,0:T(8,128)}, u32[]{:S(2)}) copy-start(s32[4,2,8,128]{3,2,1,0:T(8,128)} %get-tuple-element.46.refs_0_) | copy-start | bytes 98308
  297.0 74.1 %copy-start.9 = (s32[4,2,8,128]{3,2,1,0:T(8,128)S(1)}, s32[4,2,8,128]{3,2,1,0:T(8,128)}, u32[]{:S(2)}) copy-start(s32[4,2,8,128]{3,2,1,0:T(8,128)} %get-tuple-element.47.refs_1_) | copy-start | bytes 98308
  297.0 74.1 %copy-start.11 = (s32[4,2,8,128]{3,2,1,0:T(8,128)S(1)}, s32[4,2,8,128]{3,2,1,0:T(8,128)}, u32[]{:S(2)}) copy-start(s32[4,2,8,128]{3,2,1,0:T(8,128)} %get-tuple-element.48.refs_2_) | copy-start | bytes 98308
  371.1 0.8 copy-start.12
  371.9 0.8 copy-start.13
  372.6 0.8 copy-start.14
  395.1 1.5 copy-start.1
  396.6 1.5 copy-start.2

commit v4 on v0

v4 whole, which is shorter than its diff:
```python
import functools

import jax
import jax.numpy as jnp
from jax import lax
from jax.experimental import pallas as pl
from jax.experimental.pallas import tpu as pltpu
from jax.sharding import PartitionSpec as P

MESH = pl.DeviceIdType.MESH
LANES = 16
RING = 4
STRIDE = {'x': 1, 'y': RING, 'z': RING * RING}
ORDERS = ('xyz', 'yzx', 'zxy')
STREAMS = range(2)
PARTS = range(3)
WIDTHS = ((640, 640, 768), (768, 640, 640))
STARTS = ((0, 640, 1280), (0, 768, 1408))
SPAN = 768
SPAN_STARTS = (0, 640, 1280)
BOTH = [(q, r) for q in STREAMS for r in PARTS]


class Place:
    def __init__(self):
        self.core, self.chip = lax.axis_index('ep2'), lax.axis_index('ep')
        self.other = 1 - self.core
        self.coord = {axis: lax.rem(self.chip // stride, RING) for axis, stride in STRIDE.items()}

    def pos(self, axis, step):
        return lax.rem(self.coord[axis] + step + RING, RING)

    def at(self, axis, step):
        return self.chip + (self.pos(axis, step) - self.coord[axis]) * STRIDE[axis]

    def greet(self, both_cores):
        barrier = pltpu.get_barrier_semaphore()
        peers = [(self.other, self.chip)]
        for axis in STRIDE:
            for step in (1, -1):
                peers += [(c, self.at(axis, step)) for c in ((self.core, self.other) if both_cores else (self.core,))]
        for c, chip in peers:
            pl.semaphore_signal(barrier, inc=1, device_id=(0, c, chip), device_id_type=MESH)
        pl.semaphore_wait(barrier, len(peers))


class Lane:
    def __init__(self, place, axis, source, target, relay, send, recv, index, switch=False):
        self.place, self.axis, self.source, self.target, self.relay = place, axis, source, target, relay
        self.send, self.recv, self.index, self.switch = send, recv, index, switch
        self.sent = []

    def start(self, src, dst, s, r, core, chip):
        copy = pltpu.make_async_remote_copy(src_ref=src, dst_ref=dst, send_sem=self.send.at[self.index, s], recv_sem=self.recv.at[self.index, r], device_id=(0, core, chip), device_id_type=MESH)
        copy.start()
        self.sent.append(copy)

    def landed(self, dst, r):
        pltpu.make_async_remote_copy(src_ref=dst, dst_ref=dst, send_sem=self.send.at[self.index, 0], recv_sem=self.recv.at[self.index, r], device_id=(0, self.place.core, self.place.chip), device_id_type=MESH).wait_recv()

    def far(self):
        p = self.place
        for h, step in ((0, 1), (1, -1)):
            self.start(self.source(p.pos(self.axis, 2), h), self.relay.at[h], h, h, p.core, p.at(self.axis, step))

    def near(self):
        p = self.place
        me = p.coord[self.axis]
        for d, step in ((0, 1), (1, -1)):
            for h in (0, 1):
                k, c = (p.core, h) if self.switch else (h, p.core)
                self.start(self.source(p.pos(self.axis, step), h), self.target(me, k), 2 + 2 * d + h, 2 + 2 * d + k, c, p.at(self.axis, step))
        if self.switch:
            self.start(self.source(me, p.other), self.target(me, p.core), 8, 8, p.other, p.chip)

    def forward(self):
        p = self.place
        for h, step in ((0, 1), (1, -1)):
            self.landed(self.relay.at[h], h)
            k, c, r = (p.core, h, 6 + p.core) if self.switch else (h, p.core, 6 + h)
            self.start(self.relay.at[h], self.target(p.pos(self.axis, -step), k), 6 + h, r, c, p.at(self.axis, step))

    def arrive(self):
        p = self.place
        for d, step in ((0, -1), (1, 1)):
            for k in (0, 1):
                self.landed(self.target(p.pos(self.axis, step), k), 2 + 2 * d + k)
        for k in (0, 1):
            self.landed(self.target(p.pos(self.axis, 2), k), 6 + k)
        if self.switch:
            self.landed(self.target(p.coord[self.axis], p.other), 8)

    def own(self, local):
        p = self.place
        me = p.coord[self.axis]
        halves = [(p.core, p.core)] if self.switch else [(0, 0), (1, 1)]
        copies = [pltpu.make_async_copy(self.source(me, h), self.target(me, k), local.at[self.index, n]) for n, (h, k) in enumerate(halves)]
        for copy in copies:
            copy.start()
        return copies

    def drain(self):
        for copy in self.sent:
            copy.wait_send()


class Gather(Lane):
    def forward(self):
        p = self.place
        for h, step in ((0, 1), (1, -1)):
            part = self.target(p.pos(self.axis, -step), h)
            self.landed(part, 2 + 2 * h + h)
            self.start(part, part, 6 + h, 6 + h, p.core, p.at(self.axis, step))

    def arrive_near(self):
        p = self.place
        self.landed(self.target(p.pos(self.axis, -1), 1), 3)
        self.landed(self.target(p.pos(self.axis, 1), 0), 4)

    def arrive_far(self):
        for h in (0, 1):
            self.landed(self.target(self.place.pos(self.axis, 2), h), 6 + h)


def run(lanes, *steps):
    for step in steps:
        for lane in lanes:
            getattr(lane, step)()


def take(refs, *counts):
    refs = list(refs)
    for count in counts:
        yield refs[:count]
        del refs[:count]


def spot(axis, order, index):
    return (slice(None),) * [a for a in 'zyx' if a in order].index(axis) + (index,)


def plane_slots(shape, order, place, q):
    row = lax.broadcasted_iota(jnp.int32, shape, 0)
    first, second, third = [STRIDE[axis] for axis in order]
    dev = ((row >> 6) & 1) * RING**3 + (row >> 7) * second + ((row >> 4) & (RING - 1)) * third + place.coord[order[0]] * first
    return dev * (2 * LANES) + q * LANES + (row & (LANES - 1))


def route_kernel(ids_ref, slot_ref, count_ref):
    ids = ids_ref[...]
    n_top, n_tok = ids.shape
    experts = 2 * count_ref.shape[2]
    expert_of = lax.broadcasted_iota(jnp.int32, (experts, n_tok), 0)
    member = jnp.zeros((experts, n_tok), jnp.float32)
    for j in range(n_top):
        member = jnp.where(expert_of == ids[j:j + 1], 1.0, member)
    row = lax.broadcasted_iota(jnp.int32, (n_tok, n_tok), 0)
    col = lax.broadcasted_iota(jnp.int32, (n_tok, n_tok), 1)
    earlier = jnp.where(row < col, 1.0, 0.0).astype(jnp.bfloat16)
    member_lp = member.astype(jnp.bfloat16)
    before = jnp.dot(member_lp, earlier, preferred_element_type=jnp.float32)
    ones = jnp.ones((n_top, n_tok), jnp.bfloat16)
    counts = lax.dot_general(ones, member_lp, (((1,), (1,)), ((), ())), preferred_element_type=jnp.float32).astype(jnp.int32)
    half = n_tok // 2
    for h in (0, 1):
        count_ref[h] = counts[:, h * half:(h + 1) * half]
    for j in range(n_top):
        rank = jnp.sum(jnp.where(expert_of == ids[j:j + 1], before, 0.0), axis=0, keepdims=True)
        slot = ids[j:j + 1] * LANES + rank.astype(jnp.int32)
        for h in (0, 1):
            slot_ref[h, j:j + 1, :] = slot[:, h * half:(h + 1) * half]


def send_kernel(*refs):
    (x, slot, count), mids, (count_y,), tokens, slots, (count_x,), rows, relays, (send, recv, local) = take(refs, 3, 6, 1, 3, 3, 1, 6, 6, 3)
    place = Place()
    n_tok = x.shape[0]
    half = n_tok // 2
    cut = lambda r: pl.ds(SPAN_STARTS[r], SPAN)
    lane = functools.partial(Lane, place, send=send, recv=recv)
    gather = functools.partial(Gather, place, relay=None, send=send, recv=recv)
    first = [gather(axis=ORDERS[r][0], index=r, source=lambda p, h, r=r: x.at[pl.ds(h * half, half), cut(r)],
                    target=lambda o, k, r=r: tokens[r].at[o, pl.ds(k * half, half)]) for r in PARTS]
    small = [gather(axis=ORDERS[r][0], index=3 + r, source=lambda p, h: slot.at[h], target=lambda o, k, r=r: slots[r].at[o, k]) for r in PARTS]
    small.append(gather(axis='x', index=6, source=lambda p, h: count.at[h], target=lambda o, k: count_x.at[o, k]))
    along_y = gather(axis='y', index=7, source=lambda p, h: count_x.at[:, h], target=lambda o, k: count_y.at[o, :, k])
    second = [lane(axis=ORDERS[r][1], index=8 + 3 * q + r, switch=True, relay=relays[3 * q + r],
                   source=lambda p, h, i=3 * q + r: rows[i].at[p, h],
                   target=lambda o, k, i=3 * q + r, r=r: mids[i].at[(slice(None), k) + spot(ORDERS[r][1], ORDERS[r][:2], o)]) for q, r in BOTH]
    kept = [copy for item in small + first for copy in item.own(local)]
    place.greet(True)
    run(small, 'near')
    run(first, 'near')

    def pack(q, r, step):
        a = place.pos(ORDERS[r][0], step)
        n_row = 2 * RING * RING * LANES
        wanted = plane_slots((n_row, half), ORDERS[r], place, q)
        picks = []
        for h in (0, 1):
            pick = jnp.zeros((n_row, half), jnp.float32)
            for j in range(slots[r].shape[2]):
                pick = jnp.where(wanted == slots[r][a, h, j:j + 1], 1.0, pick)
            picks.append(pick.astype(jnp.bfloat16))
        offset = STARTS[q][r] - SPAN_STARTS[r]
        got = jnp.dot(jnp.concatenate(picks, axis=1), tokens[r][a, :, offset:offset + WIDTHS[q][r]], preferred_element_type=jnp.float32)
        rows[3 * q + r][:, :, :, a] = got.astype(jnp.bfloat16).reshape(RING, 2, RING, LANES, WIDTHS[q][r])

    for copy in kept:
        copy.wait()
    for r in PARTS:
        pack(0, r, 0)
    run(small, 'forward')
    run(first, 'forward')
    run(small, 'arrive_near', 'arrive_far')
    run(first, 'arrive_near')
    kept = along_y.own(local)
    run([along_y], 'near')
    for r in PARTS:
        pl.loop(0, 2)(lambda n, r=r: pack(0, r, 1 + 2 * n))
    run(first, 'arrive_far')
    for r in PARTS:
        pack(0, r, 2)
    run(second[:3], 'far', 'near')
    for r in PARTS:
        pl.loop(0, RING)(lambda n, r=r: pack(1, r, n))
    run(second[:3], 'forward')
    run(second[3:], 'far', 'near')
    run([along_y], 'forward')
    for item in second:
        kept += item.own(local)
    run(second[3:], 'forward')
    run([along_y], 'arrive_near', 'arrive_far')
    run(second, 'arrive')
    for copy in kept:
        copy.wait()
    run(small + first + [along_y] + second, 'drain')


def expert_stage_kernel(*refs):
    mids, (w_in, w_out, count_y), backs, (count_z, count_other), rows, relays, back_relays, (w_in_v, w_out_v), (send, recv, local, extra) = take(refs, 6, 3, 6, 2, 6, 6, 6, 2, 4)
    place = Place()
    lane = functools.partial(Lane, place, send=send, recv=recv)
    out = [lane(axis=ORDERS[r][2], index=3 * q + r, relay=relays[3 * q + r], source=lambda p, h, i=3 * q + r: mids[i].at[p, h],
                target=lambda o, k, i=3 * q + r, r=r: rows[i].at[(k,) + spot(ORDERS[r][2], 'zyx', o)]) for q, r in BOTH]
    back = [lane(axis=ORDERS[r][2], index=6 + 3 * q + r, relay=back_relays[3 * q + r], target=lambda o, k, i=3 * q + r: backs[i].at[o, k],
                 source=lambda p, h, i=3 * q + r, r=r: rows[i].at[(h,) + spot(ORDERS[r][2], 'zyx', p)]) for q, r in BOTH]
    along_z = Gather(place, 'z', lambda p, h: count_y.at[:, :, h], lambda o, k: count_z.at[o, :, :, k], None, send, recv, 12)
    loads = [pltpu.make_async_copy(w_in, w_in_v, extra.at[0]), pltpu.make_async_copy(w_out, w_out_v, extra.at[1])]
    own = [out[i].own(local) for i in range(6)] + [along_z.own(local)]
    for copy in loads:
        copy.start()
    place.greet(False)

    def expert(q, step):
        core, z = step // 2, 2 * lax.rem(step, 2)
        n_row = 2 * RING * RING * LANES
        total = None
        for r in PARTS:
            part = rows[3 * q + r][core, pl.ds(z, 2)].reshape(n_row, WIDTHS[q][r])
            term = jnp.dot(part, w_in_v[q, STARTS[q][r]:STARTS[q][r] + WIDTHS[q][r]], preferred_element_type=jnp.float32)
            total = term if total is None else total + term
        hidden = jax.nn.gelu(total, approximate=True).astype(jnp.bfloat16)
        for r in PARTS:
            res = jnp.dot(hidden, w_out_v[q, :, STARTS[q][r]:STARTS[q][r] + WIDTHS[q][r]], preferred_element_type=jnp.float32)
            rows[3 * q + r][core, pl.ds(z, 2)] = res.astype(jnp.bfloat16).reshape(2, RING, RING, LANES, WIDTHS[q][r])

    run(out[:3], 'far', 'near')
    run([along_z], 'near')
    run(out[:3], 'forward')
    run(out[3:], 'far', 'near')
    run([along_z], 'forward', 'arrive_near', 'arrive_far')
    for copy in own[6]:
        copy.wait()
    swap = Lane(place, 'z', None, None, None, send, recv, 13)
    swap.start(count_z, count_other, 0, 0, place.other, place.chip)
    for copy in loads:
        copy.wait()
    kept = []
    for q in STREAMS:
        mine, behind = slice(3 * q, 3 * q + 3), (out[3:], back[:3])[q]
        run(out[mine], 'arrive')
        for copies in own[mine]:
            for copy in copies:
                copy.wait()
        pl.loop(0, 3)(lambda n, q=q: expert(q, n))
        run(behind, 'forward')
        expert(q, 3)
        run(back[mine], 'far', 'near')
        for item in back[mine]:
            kept += item.own(local)
    run(back[3:], 'forward')
    swap.landed(count_other, 0)
    run(back, 'arrive')
    for copy in kept:
        copy.wait()
    run(out + back + [along_z, swap], 'drain')


def weight_kernel(capacity, ids_ref, slot_ref, gate_ref, mine_ref, partner_ref, out_ref):
    place = Place()
    ids, gate = ids_ref[...], gate_ref[...]
    n_top, n_tok = ids.shape
    mine = mine_ref[...]
    ahead = lax.broadcasted_iota(jnp.int32, mine.shape, 0) < place.chip
    off = jnp.sum(jnp.where(ahead, mine, 0), axis=0) + jnp.where(place.core == 1, jnp.sum(partner_ref[...], axis=0), 0)
    off = jnp.concatenate([off[0], off[1]], axis=1)
    high = (off >> 7).astype(jnp.bfloat16)
    low = (off & 127).astype(jnp.bfloat16)
    expert_of = lax.broadcasted_iota(jnp.int32, (off.shape[1], n_tok), 0)
    half = n_tok // 2
    for j in range(n_top):
        choice = jnp.where(expert_of == ids[j:j + 1], 1.0, 0.0).astype(jnp.bfloat16)
        first = 128 * jnp.dot(high, choice, preferred_element_type=jnp.float32) + jnp.dot(low, choice, preferred_element_type=jnp.float32)
        first = first[0:1].astype(jnp.int32)
        for h in (0, 1):
            cut = slice(h * half, (h + 1) * half)
            rank = first[:, cut] + slot_ref[h, j:j + 1] - ids[j:j + 1, cut] * LANES
            out_ref[h, j:j + 1] = jnp.where(rank < capacity, gate[j:j + 1, cut], 0.0)


def return_kernel(*refs):
    mids, (slot, gate, x, y), rows, relays, slots, gates, sums, got, sum_relays, (send, recv, local) = take(refs, 6, 4, 6, 6, 3, 3, 3, 3, 3, 3)
    place = Place()
    n_tok = x.shape[0]
    half = n_tok // 2
    lane = functools.partial(Lane, place, send=send, recv=recv)
    gather = functools.partial(Gather, place, relay=None, send=send, recv=recv)
    small = [gather(axis=ORDERS[r][0], index=r, source=lambda p, h: slot.at[h], target=lambda o, k, r=r: slots[r].at[o, k]) for r in PARTS]
    small += [gather(axis=ORDERS[r][0], index=3 + r, source=lambda p, h: gate.at[h], target=lambda o, k, r=r: gates[r].at[o, k]) for r in PARTS]
    second = [lane(axis=ORDERS[r][1], index=6 + 3 * q + r, switch=True, relay=relays[3 * q + r], target=lambda o, k, i=3 * q + r: rows[i].at[o, k],
                   source=lambda p, h, i=3 * q + r, r=r: mids[i].at[(slice(None), h) + spot(ORDERS[r][1], ORDERS[r][:2], p)]) for q, r in BOTH]
    first = [lane(axis=ORDERS[r][0], index=12 + r, relay=sum_relays[r], source=lambda p, h, r=r: sums[r].at[p, pl.ds(h * half, half)],
                  target=lambda o, k, r=r: got[r].at[o, pl.ds(k * half, half)]) for r in PARTS]
    kept = [copy for item in small + second for copy in item.own(local)]
    place.greet(True)
    run(small, 'near')
    run(second[:3], 'far', 'near')
    for r in PARTS:
        sums[r][...] = jnp.zeros_like(sums[r])
    run(small, 'forward', 'arrive_near', 'arrive_far')
    run(second[:3], 'forward')
    run(second[3:], 'far', 'near')
    for copy in kept:
        copy.wait()

    def combine(q, r, step, h):
        a = place.pos(ORDERS[r][0], step)
        n_row = 2 * RING * RING * LANES
        wanted = plane_slots((n_row, half), ORDERS[r], place, q)
        weight = jnp.zeros((n_row, half), jnp.float32)
        for j in range(slots[r].shape[2]):
            weight = jnp.where(wanted == slots[r][a, h, j:j + 1], gates[r][a, h, j:j + 1], weight)
        high = weight.astype(jnp.bfloat16)
        rest = weight - high.astype(jnp.float32)
        mid = rest.astype(jnp.bfloat16)
        low = (rest - mid.astype(jnp.float32)).astype(jnp.bfloat16)
        weights = jnp.concatenate([high, mid, low], axis=1)
        back = rows[3 * q + r][:, :, :, a].reshape(n_row, WIDTHS[q][r])
        mix = lax.dot_general(weights, back, (((0,), (0,)), ((), ())), preferred_element_type=jnp.float32)
        offset = STARTS[q][r] - SPAN_STARTS[r]
        sums[r][a, pl.ds(pl.multiple_of(h * half, half), half), offset:offset + WIDTHS[q][r]] += mix[:half] + mix[half:2 * half] + mix[2 * half:]

    run(second[:3], 'arrive')
    for r in PARTS:
        pl.loop(0, 2 * RING)(lambda n, r=r: combine(0, r, n // 2, lax.rem(n, 2)))
    run(second[3:], 'forward', 'arrive')
    for r in PARTS:
        pl.loop(0, 2)(lambda h, r=r: combine(1, r, 2, h))
    run(first, 'far')
    for r in PARTS:
        pl.loop(0, 4)(lambda n, r=r: combine(1, r, 1 + 2 * (n // 2), lax.rem(n, 2)))
    run(first, 'near', 'forward')
    for r in PARTS:
        pl.loop(0, 2)(lambda h, r=r: combine(1, r, 0, h))
    run(first, 'arrive')
    for c in range(0, x.shape[1], 128):
        total = x[:, c:c + 128].astype(jnp.float32)
        for r in PARTS:
            if SPAN_STARTS[r] <= c < SPAN_STARTS[r] + SPAN:
                cut = slice(c - SPAN_STARTS[r], c - SPAN_STARTS[r] + 128)
                total += sums[r][place.coord[ORDERS[r][0]], :, cut]
                for step in (1, 2, 3):
                    total += got[r][place.pos(ORDERS[r][0], step), :, cut]
        y[:, c:c + 128] = total.astype(y.dtype)
    run(small + second + first, 'drain')


def solution(mesh):
    dev_axes = ('ep2', 'ep')
    bf16, f32, i32 = jnp.bfloat16, jnp.float32, jnp.int32
    group_size = mesh.shape['ep2'] * mesh.shape['ep']
    anywhere, dma = pl.BlockSpec(memory_space=pl.ANY), pltpu.SemaphoreType.DMA
    block = (RING, RING, LANES)
    vmem = lambda shapes, dtype: [pltpu.VMEM(shape, dtype) for shape in shapes]
    per_part = lambda lead: [lead + (WIDTHS[q][r],) for q, r in BOTH]
    params = lambda n: pltpu.CompilerParams(collective_id=n, has_side_effects=True, vmem_limit_bytes=60 * 2**20)

    def local_step(x, ids, gate, w_a, w_b):
        n_tok, d_model = x.shape
        n_top = ids.shape[1]
        experts = w_a.shape[0] * group_size
        capacity = 8 * ((5 * group_size * n_tok * n_top) // (32 * experts))
        small = (2, n_top, n_tok // 2)
        ids_t, gate_t = ids.T, gate.T
        shape = jax.ShapeDtypeStruct
        slot, counts = pl.pallas_call(route_kernel, out_shape=(shape(small, i32), shape((2, n_top, experts // 2), i32)), name='route')(ids_t)
        *mids, count_y = pl.pallas_call(
            send_kernel,
            in_specs=[anywhere] * 3,
            out_specs=[anywhere] * 7,
            out_shape=[shape(s, bf16) for s in per_part((RING, 2) + block)] + [shape((RING, RING) + small, i32)],
            scratch_shapes=vmem([(RING, n_tok, SPAN)] * 3, bf16) + vmem([(RING,) + small] * 4, i32)
            + vmem(per_part((RING, 2) + block), bf16) + vmem(per_part((2,) + block), bf16) + [dma((14, 9)), dma((14, 9)), dma((14, 2))],
            compiler_params=params(0),
            name='send_stage',
        )(x, slot, counts)
        chips = (RING, RING, RING) + small
        *mids, count_z, count_other = pl.pallas_call(
            expert_stage_kernel,
            in_specs=[anywhere] * 9,
            out_specs=[anywhere] * 8,
            out_shape=[shape(s, bf16) for s in per_part((RING, 2) + block)] + [shape(chips, i32)] * 2,
            scratch_shapes=vmem(per_part((2, RING) + block), bf16) + vmem(per_part((2,) + block), bf16) * 2
            + vmem([w_a.shape, w_b.shape], bf16) + [dma((14, 9)), dma((14, 9)), dma((14, 2)), dma((2,))],
            compiler_params=params(1),
            name='expert_stage',
        )(*mids, w_a, w_b, count_y)
        chips = (RING**3,) + small
        gates = pl.pallas_call(functools.partial(weight_kernel, capacity), out_shape=shape(small, f32), name='weight')(
            ids_t, slot, gate_t, count_z.reshape(chips), count_other.reshape(chips))
        return pl.pallas_call(
            return_kernel,
            in_specs=[anywhere] * 8 + [pl.BlockSpec(memory_space=pltpu.VMEM)],
            out_specs=pl.BlockSpec(memory_space=pltpu.VMEM),
            out_shape=shape(x.shape, x.dtype),
            scratch_shapes=vmem(per_part((RING, 2) + block), bf16) + vmem(per_part((2,) + block), bf16)
            + vmem([(RING,) + small] * 3, i32) + vmem([(RING,) + small] * 3, f32) + vmem([(RING, n_tok, SPAN)] * 6, f32)
            + vmem([(2, n_tok // 2, SPAN)] * 3, f32) + [dma((15, 9)), dma((15, 9)), dma((15, 2))],
            compiler_params=params(2),
            name='return_stage',
        )(*mids, slot, gates, x)

    tok_spec = P(('dp', 'ep2', 'ep'), None)
    w_spec = P(dev_axes, None, None)
    return jax.shard_map(local_step, mesh=mesh, in_specs=(tok_spec, tok_spec, tok_spec, w_spec, w_spec), out_specs=tok_spec, check_vma=False)
```

time: 901 us -> 362 us (0.40)
  the two profiles are of different devices: /device:TPU:8 before, /device:TPU:1 now
where the time goes in v4:
time: 362 us; the launch traced here: 361 us
  Pallas kernels  359 us (99%)
    pallas_call x1, Pallas kernels, local_step(): pl.pallas_call(expert_stage_kernel, in_specs=[anywhere] * 9, out_specs=[a...  143 us
    pallas_call x1, Pallas kernels, local_step(): pl.pallas_call(return_kernel, in_specs=[anywhere] * 8 + [pl.BlockSpec(mem...  120 us
    pallas_call x1, Pallas kernels, local_step(): pl.pallas_call(send_kernel, in_specs=[anywhere] * 3, out_specs=[anywhere]...  91.3 us

profile of v4, /device:TPU:1, one launch (start us, length us, event | category | flops | bytes accessed | tf_op | source)
XLA Modules:
  0.0 361.3 jit_solution(2630233424383606721)
XLA Ops:
  0.0 1.8 route.1
  1.8 91.3 %send_stage.1 = (bf16[4,2,4,4,16,640]{5,4,3,2,1,0:T(8,128)(2,1)}, bf16[4,2,4,4,16,640]{5,4,3,2,1,0:T(8,128)(2,1)}, bf16[4,2,4,4,16,768]{5,4,3,2,1,0:T(8,128)(2,1...) custom-call(bf16[256,2048]{1,0:T(8,128)(2,1)} %refs_8_.1, ...), custom_call_target="tpu_custom_call" | custom-call | tf_op jit(solution)/shard_map/send_stage/pallas_call | solution.py:408
  93.1 143.2 %expert_stage.1 = (bf16[4,2,4,4,16,640]{5,4,3,2,1,0:T(8,128)(2,1)}, bf16[4,2,4,4,16,640]{5,4,3,2,1,0:T(8,128)(2,1)}, bf16[4,2,4,4,16,768]{5,4,3,2,1,0:T(8,128)(2...) custom-call(bf16[4,2,4,4,16,640]{5,4,3,2,1,0:T(8,128)(2,1)} %get-tup, ...), custom_call_target="tpu_custom_call" | custom-call | tf_op jit(solution)/shard_map/expert_stage/pallas_call | solution.py:419
  236.3 2.3 weight.1.refs_7_
  238.7 120.3 %return_stage.1 = bf16[256,2048]{1,0:T(8,128)(2,1)} custom-call(bf16[4,2,4,4,16,640]{5,4,3,2,1,0:T(8,128)(2,1)} %get-tuple-element.31.refs_0_, bf16[4,2,4,4,16,640]{5,4,3,2,1,0:T(8,128)(2,1)} %get-tuple-element.32.refs_1_, bf16[4,2,4,4,16,768]{5,4,3,2,1,0:T(8,128)(2,1)} %get-tuple-element.33.refs_2_, ...), custom_call_target="tpu_custom_call" | custom-call | tf_op jit(solution)/shard_map/return_stage/pallas_call | solution.py:432
  359.0 2.3 copy.7

commit v5 on v4

v5 whole, which is shorter than its diff:
```python
import functools

import jax
import jax.numpy as jnp
from jax import lax
from jax.experimental import pallas as pl
from jax.experimental.pallas import tpu as pltpu
from jax.sharding import PartitionSpec as P

MESH = pl.DeviceIdType.MESH
LANES = 16
RING = 4
STRIDE = {'x': 1, 'y': RING, 'z': RING * RING}
ORDERS = ('xyz', 'yzx', 'zxy')
STREAMS = range(2)
PARTS = range(3)
WIDTHS = ((640, 640, 768), (768, 640, 640))
STARTS = ((0, 640, 1280), (0, 768, 1408))
SPAN = 768
SPAN_STARTS = (0, 640, 1280)
BOTH = [(q, r) for q in STREAMS for r in PARTS]


class Place:
    def __init__(self):
        self.core, self.chip = lax.axis_index('ep2'), lax.axis_index('ep')
        self.other = 1 - self.core
        self.coord = {axis: lax.rem(self.chip // stride, RING) for axis, stride in STRIDE.items()}

    def pos(self, axis, step):
        return lax.rem(self.coord[axis] + step + RING, RING)

    def at(self, axis, step):
        return self.chip + (self.pos(axis, step) - self.coord[axis]) * STRIDE[axis]

    def greet(self, both_cores):
        barrier = pltpu.get_barrier_semaphore()
        peers = [(self.other, self.chip)]
        for axis in STRIDE:
            for step in (1, -1):
                peers += [(c, self.at(axis, step)) for c in ((self.core, self.other) if both_cores else (self.core,))]
        for c, chip in peers:
            pl.semaphore_signal(barrier, inc=1, device_id=(0, c, chip), device_id_type=MESH)
        pl.semaphore_wait(barrier, len(peers))


class Lane:
    def __init__(self, place, axis, source, target, relay, send, recv, index, switch=False):
        self.place, self.axis, self.source, self.target, self.relay = place, axis, source, target, relay
        self.send, self.recv, self.index, self.switch = send, recv, index, switch
        self.sent = []

    def start(self, src, dst, s, r, core, chip):
        copy = pltpu.make_async_remote_copy(src_ref=src, dst_ref=dst, send_sem=self.send.at[self.index, s], recv_sem=self.recv.at[self.index, r], device_id=(0, core, chip), device_id_type=MESH)
        copy.start()
        self.sent.append(copy)

    def landed(self, dst, r):
        pltpu.make_async_remote_copy(src_ref=dst, dst_ref=dst, send_sem=self.send.at[self.index, 0], recv_sem=self.recv.at[self.index, r], device_id=(0, self.place.core, self.place.chip), device_id_type=MESH).wait_recv()

    def far(self):
        p = self.place
        for h, step in ((0, 1), (1, -1)):
            self.start(self.source(p.pos(self.axis, 2), h), self.relay.at[h], h, h, p.core, p.at(self.axis, step))

    def near(self):
        p = self.place
        me = p.coord[self.axis]
        for d, step in ((0, 1), (1, -1)):
            for h in (0, 1):
                k, c = (p.core, h) if self.switch else (h, p.core)
                self.start(self.source(p.pos(self.axis, step), h), self.target(me, k), 2 + 2 * d + h, 2 + 2 * d + k, c, p.at(self.axis, step))
        if self.switch:
            self.start(self.source(me, p.other), self.target(me, p.core), 8, 8, p.other, p.chip)

    def forward(self):
        p = self.place
        for h, step in ((0, 1), (1, -1)):
            self.landed(self.relay.at[h], h)
            k, c, r = (p.core, h, 6 + p.core) if self.switch else (h, p.core, 6 + h)
            self.start(self.relay.at[h], self.target(p.pos(self.axis, -step), k), 6 + h, r, c, p.at(self.axis, step))

    def arrive(self):
        p = self.place
        for d, step in ((0, -1), (1, 1)):
            for k in (0, 1):
                self.landed(self.target(p.pos(self.axis, step), k), 2 + 2 * d + k)
        for k in (0, 1):
            self.landed(self.target(p.pos(self.axis, 2), k), 6 + k)
        if self.switch:
            self.landed(self.target(p.coord[self.axis], p.other), 8)

    def own(self, local):
        p = self.place
        me = p.coord[self.axis]
        halves = [(p.core, p.core)] if self.switch else [(0, 0), (1, 1)]
        copies = [pltpu.make_async_copy(self.source(me, h), self.target(me, k), local.at[self.index, n]) for n, (h, k) in enumerate(halves)]
        for copy in copies:
            copy.start()
        return copies

    def drain(self):
        for copy in self.sent:
            copy.wait_send()


class Gather(Lane):
    def forward(self):
        p = self.place
        for h, step in ((0, 1), (1, -1)):
            part = self.target(p.pos(self.axis, -step), h)
            self.landed(part, 2 + 2 * h + h)
            self.start(part, part, 6 + h, 6 + h, p.core, p.at(self.axis, step))

    def arrive_near(self):
        p = self.place
        self.landed(self.target(p.pos(self.axis, -1), 1), 3)
        self.landed(self.target(p.pos(self.axis, 1), 0), 4)

    def arrive_far(self):
        for h in (0, 1):
            self.landed(self.target(self.place.pos(self.axis, 2), h), 6 + h)


class Reduce(Lane):
    def near(self):
        p = self.place
        for side, step in ((0, 1), (1, -1)):
            self.start(self.source(p.pos(self.axis, step), 1 - side), self.target(side, 1 - side), 2 + side, 2 + side, p.core, p.at(self.axis, step))

    def add(self):
        for h, step in ((0, 1), (1, -1)):
            self.landed(self.relay.at[h], h)
            self.relay[h] += self.source(self.place.pos(self.axis, step), h)[...]

    def forward(self):
        p = self.place
        for h, step in ((0, 1), (1, -1)):
            self.start(self.relay.at[h], self.target(h, h), 4 + h, 4 + h, p.core, p.at(self.axis, step))

    def arrive(self):
        for side in (0, 1):
            self.landed(self.target(side, 1 - side), 2 + side)
            self.landed(self.target(side, side), 4 + side)


def run(lanes, *steps):
    for step in steps:
        for lane in lanes:
            getattr(lane, step)()


def take(refs, *counts):
    refs = list(refs)
    for count in counts:
        yield refs[:count]
        del refs[:count]


def spot(axis, order, index):
    return (slice(None),) * [a for a in 'zyx' if a in order].index(axis) + (index,)


def plane_slots(shape, order, place, q, base=0):
    row = lax.broadcasted_iota(jnp.int32, shape, 0) + base
    first, second, third = [STRIDE[axis] for axis in order]
    dev = ((row >> 6) & 1) * RING**3 + (row >> 7) * second + ((row >> 4) & (RING - 1)) * third + place.coord[order[0]] * first
    return dev * (2 * LANES) + q * LANES + (row & (LANES - 1))


def route_kernel(ids_ref, slot_ref, count_ref):
    ids = ids_ref[...]
    n_top, n_tok = ids.shape
    experts = 2 * count_ref.shape[2]
    expert_of = lax.broadcasted_iota(jnp.int32, (experts, n_tok), 0)
    member = jnp.zeros((experts, n_tok), jnp.float32)
    for j in range(n_top):
        member = jnp.where(expert_of == ids[j:j + 1], 1.0, member)
    row = lax.broadcasted_iota(jnp.int32, (n_tok, n_tok), 0)
    col = lax.broadcasted_iota(jnp.int32, (n_tok, n_tok), 1)
    earlier = jnp.where(row < col, 1.0, 0.0).astype(jnp.bfloat16)
    member_lp = member.astype(jnp.bfloat16)
    before = jnp.dot(member_lp, earlier, preferred_element_type=jnp.float32)
    ones = jnp.ones((n_top, n_tok), jnp.bfloat16)
    counts = lax.dot_general(ones, member_lp, (((1,), (1,)), ((), ())), preferred_element_type=jnp.float32).astype(jnp.int32)
    half = n_tok // 2
    for h in (0, 1):
        count_ref[h] = counts[:, h * half:(h + 1) * half]
    for j in range(n_top):
        rank = jnp.sum(jnp.where(expert_of == ids[j:j + 1], before, 0.0), axis=0, keepdims=True)
        slot = ids[j:j + 1] * LANES + rank.astype(jnp.int32)
        for h in (0, 1):
            slot_ref[h, j:j + 1, :] = slot[:, h * half:(h + 1) * half]


def layer_kernel(capacity, *refs):
    (x, ids, gate, slot, count), (w_in, w_out), (y,), mids, backs, ends, b_relay, c_relay, cb_relay, bb_relay, refs = take(refs, 5, 2, 1, 6, 6, 6, 6, 6, 6, 6, None)
    tokens, slots, gates, packed, rows, sums, got, sum_relay, (count_x, count_y, count_z, count_other, mine, w_in_v, w_out_v, send, recv, local, extra) = take(refs, 3, 3, 3, 6, 6, 3, 3, 3, None)
    place = Place()
    n_tok, n_top = x.shape[0], slot.shape[1]
    half = n_tok // 2
    n_row = 2 * RING * RING * LANES
    index = iter(range(send.shape[0]))
    lane = lambda kind, axis, source, target, relay=None, switch=False: kind(place, axis, source, target, relay, send, recv, next(index), switch)
    first, second, third = [[ORDERS[r][k] for r in PARTS] for k in PARTS]

    a_small = [lane(Gather, first[r], lambda p, h: slot.at[h], lambda o, k, r=r: slots[r].at[o, k]) for r in PARTS]
    a_small.append(lane(Gather, 'x', lambda p, h: count.at[h], lambda o, k: count_x.at[o, k]))
    a_out = [lane(Gather, first[r], lambda p, h, r=r: x.at[pl.ds(h * half, half), pl.ds(SPAN_STARTS[r], SPAN)],
                  lambda o, k, r=r: tokens[r].at[o, pl.ds(k * half, half)]) for r in PARTS]
    along_y = lane(Gather, 'y', lambda p, h: count_x.at[:, h], lambda o, k: count_y.at[o, :, k])
    along_z = lane(Gather, 'z', lambda p, h: count_y.at[:, :, h], lambda o, k: count_z.at[o, :, :, k])
    swap = lane(Lane, 'z', None, None)
    a_gate = [lane(Gather, first[r], lambda p, h: mine.at[h], lambda o, k, r=r: gates[r].at[o, k]) for r in PARTS]
    b_out = [lane(Lane, second[r], lambda p, h, i=3 * q + r: packed[i].at[p, h],
                  lambda o, k, i=3 * q + r, r=r: mids[i].at[(slice(None), k) + spot(second[r], ORDERS[r][:2], o)], b_relay[3 * q + r], True) for q, r in BOTH]
    c_out = [lane(Lane, third[r], lambda p, h, i=3 * q + r: mids[i].at[p, h],
                  lambda o, k, i=3 * q + r, r=r: rows[i].at[(k,) + spot(third[r], 'zyx', o)], c_relay[3 * q + r]) for q, r in BOTH]
    c_back = [lane(Lane, third[r], lambda p, h, i=3 * q + r, r=r: rows[i].at[(h,) + spot(third[r], 'zyx', p)],
                   lambda o, k, i=3 * q + r: backs[i].at[o, k], cb_relay[3 * q + r]) for q, r in BOTH]
    b_back = [lane(Lane, second[r], lambda p, h, i=3 * q + r, r=r: backs[i].at[(slice(None), h) + spot(second[r], ORDERS[r][:2], p)],
                   lambda o, k, i=3 * q + r: ends[i].at[o, k], bb_relay[3 * q + r], True) for q, r in BOTH]
    a_back = [lane(Reduce, first[r], lambda p, h, r=r: sums[r].at[p, pl.ds(h * half, half)],
                   lambda side, h, r=r: got[r].at[side, pl.ds(h * half, half)], sum_relay[r]) for r in PARTS]
    one, two = slice(0, 3), slice(3, 6)

    def pack(q, r, step):
        a = place.pos(first[r], step)
        offset = STARTS[q][r] - SPAN_STARTS[r]
        for part in (0, 1):
            wanted = plane_slots((n_row // 2, half), ORDERS[r], place, q, part * n_row // 2)
            picks = []
            for h in (0, 1):
                pick = jnp.zeros((n_row // 2, half), jnp.float32)
                for j in range(n_top):
                    pick = jnp.where(wanted == slots[r][a, h, j:j + 1], 1.0, pick)
                picks.append(pick.astype(jnp.bfloat16))
            block = jnp.dot(jnp.concatenate(picks, axis=1), tokens[r][a, :, offset:offset + WIDTHS[q][r]], preferred_element_type=jnp.float32)
            packed[3 * q + r][2 * part:2 * part + 2, :, :, a] = block.astype(jnp.bfloat16).reshape(RING // 2, 2, RING, LANES, WIDTHS[q][r])

    def expert(q, step):
        core, z = step // RING, lax.rem(step, RING)
        total = None
        for r in PARTS:
            part = rows[3 * q + r][core, z].reshape(RING * RING * LANES, WIDTHS[q][r])
            term = jnp.dot(part, w_in_v[STARTS[q][r]:STARTS[q][r] + WIDTHS[q][r]], preferred_element_type=jnp.float32)
            total = term if total is None else total + term
        hidden = jax.nn.gelu(total, approximate=True).astype(jnp.bfloat16)
        for r in PARTS:
            res = jnp.dot(hidden, w_out_v[:, STARTS[q][r]:STARTS[q][r] + WIDTHS[q][r]], preferred_element_type=jnp.float32)
            rows[3 * q + r][core, z] = res.astype(jnp.bfloat16).reshape(RING, RING, LANES, WIDTHS[q][r])

    def weigh():
        counted = lambda ref: ref[...].reshape((RING**3,) + count.shape)
        ahead = lax.broadcasted_iota(jnp.int32, (RING**3,) + count.shape, 0) < place.chip
        off = jnp.sum(jnp.where(ahead, counted(count_z), 0), axis=0) + jnp.where(place.core == 1, jnp.sum(counted(count_other), axis=0), 0)
        off = jnp.concatenate([off[0], off[1]], axis=1)
        high, low = (off >> 7).astype(jnp.bfloat16), (off & 127).astype(jnp.bfloat16)
        expert_of = lax.broadcasted_iota(jnp.int32, (off.shape[1], n_tok), 0)
        for j in range(n_top):
            choice = jnp.where(expert_of == ids[j:j + 1], 1.0, 0.0).astype(jnp.bfloat16)
            before = 128 * jnp.dot(high, choice, preferred_element_type=jnp.float32) + jnp.dot(low, choice, preferred_element_type=jnp.float32)
            before = before[0:1].astype(jnp.int32)
            for h in (0, 1):
                cut = slice(h * half, (h + 1) * half)
                rank = before[:, cut] + slot[h, j:j + 1] - ids[j:j + 1, cut] * LANES
                mine[h, j:j + 1] = jnp.where(rank < capacity, gate[j:j + 1, cut], 0.0)

    def combine(q, r, step, h):
        a = place.pos(first[r], step)
        wanted = plane_slots((n_row, half), ORDERS[r], place, q)
        weight = jnp.zeros((n_row, half), jnp.float32)
        for j in range(n_top):
            weight = jnp.where(wanted == slots[r][a, h, j:j + 1], gates[r][a, h, j:j + 1], weight)
        high = weight.astype(jnp.bfloat16)
        rest = weight - high.astype(jnp.float32)
        mid = rest.astype(jnp.bfloat16)
        low = (rest - mid.astype(jnp.float32)).astype(jnp.bfloat16)
        weights = jnp.concatenate([high, mid, low], axis=1)
        offset = STARTS[q][r] - SPAN_STARTS[r]
        for lo, hi in ((0, 384), (384, WIDTHS[q][r])):
            back = packed[3 * q + r][:, :, :, a, :, lo:hi].reshape(n_row, hi - lo)
            mix = lax.dot_general(weights, back, (((0,), (0,)), ((), ())), preferred_element_type=jnp.float32)
            sums[r][a, pl.ds(pl.multiple_of(h * half, half), half), offset + lo:offset + hi] += mix[:half] + mix[half:2 * half] + mix[2 * half:]

    def wait(copies):
        for copy in copies:
            copy.wait()

    def own(lanes):
        return [copy for item in lanes for copy in item.own(local)]

    def load(src, dst, n):
        copy = pltpu.make_async_copy(src, dst, extra.at[n])
        copy.start()
        return copy

    def own_rows(lanes, i):
        me = [place.coord[item.axis] for item in lanes]
        return [load(item.source(me[r], place.core), packed[i + r].at[me[r], place.core], 4 + i + r) for r, item in enumerate(lanes)]

    def fetch(i):
        axis = second[i % 3]
        pieces = [(place.pos(axis, step),) for step in (1, 2, 3)] + [(place.coord[axis], place.other)]
        return [load(ends[i].at[at], packed[i].at[at], 10 + 4 * i + n) for n, at in enumerate(pieces)]

    kept = own(a_small + a_out)
    weights = [load(w_in.at[0], w_in_v, 0), load(w_out.at[0], w_out_v, 1)]
    place.greet(True)
    run(a_small, 'near')
    run(a_out, 'near')
    wait(kept)
    for r in PARTS:
        pack(0, r, 0)
    run(a_small, 'forward')
    run(a_out, 'forward')
    run(a_small, 'arrive_near', 'arrive_far')
    run(a_out, 'arrive_near')
    for r in PARTS:
        pl.loop(0, 2)(lambda n, r=r: pack(0, r, 1 + 2 * n))
    run(a_out, 'arrive_far')
    for r in PARTS:
        pack(0, r, 2)
    run(b_out[one], 'far', 'near')
    kept_y = own([along_y])
    run([along_y], 'near')
    kept_b = own(b_out[one])
    for r in PARTS:
        pl.loop(0, RING)(lambda n, r=r: pack(1, r, n))
    run(b_out[one], 'forward')
    run(b_out[two], 'far', 'near')
    kept_b += own(b_out[two])
    run([along_y], 'forward', 'arrive_near', 'arrive_far')
    wait(kept_y)
    kept_z = own([along_z])
    run([along_z], 'near')
    wait(kept_b)
    run(b_out[two], 'forward')
    run(b_out[one], 'arrive')
    run(c_out[one], 'far', 'near')
    kept = own(c_out[one])
    run([along_z], 'forward', 'arrive_near', 'arrive_far')
    wait(kept_z)
    swap.start(count_z, count_other, 0, 0, place.other, place.chip)
    run(c_out[one], 'forward')
    run(b_out[two], 'arrive')
    run(c_out[two], 'far', 'near')
    kept_two = own(c_out[two])
    run(c_out[one], 'arrive')
    wait(kept + weights)
    pl.loop(0, 2 * RING)(lambda n: expert(0, n))
    weights = [load(w_in.at[1], w_in_v, 2), load(w_out.at[1], w_out_v, 3)]
    run(c_out[two], 'forward')
    run(c_back[one], 'far', 'near')
    kept = own(c_back[one])
    run(c_out[two], 'arrive')
    wait(kept_two + weights)
    pl.loop(0, 2 * RING)(lambda n: expert(1, n))
    run(c_back[one], 'forward')
    run(c_back[two], 'far', 'near')
    kept_two = own(c_back[two])
    swap.landed(count_other, 0)
    weigh()
    wait(kept)
    run(c_back[two], 'forward')
    run(c_back[one], 'arrive')
    run(b_back[one], 'far', 'near')
    run(b_out, 'drain')
    kept = own_rows(b_back[one], 0)
    kept_gate = own(a_gate)
    run(a_gate, 'near')
    for r in PARTS:
        sums[r][...] = jnp.zeros_like(sums[r])
    run(a_gate, 'forward', 'arrive_near', 'arrive_far')
    wait(kept_gate + kept_two)
    run(b_back[one], 'forward')
    run(c_back[two], 'arrive')
    run(b_back[two], 'far', 'near')
    kept_two = own_rows(b_back[two], 3)
    run(b_back[one], 'arrive')
    wait(kept)
    loads = [fetch(r) for r in PARTS]
    for r in PARTS:
        wait(loads[r])
        pl.loop(0, 2 * RING)(lambda n, r=r: combine(0, r, n // 2, lax.rem(n, 2)))
    run(b_back[two], 'forward', 'arrive')
    wait(kept_two)
    loads = [fetch(3 + r) for r in PARTS]
    for r in PARTS:
        wait(loads[r])
        pl.loop(0, 2)(lambda h, r=r: combine(1, r, 2, h))
    run(a_back, 'far')
    for r in PARTS:
        pl.loop(0, 4)(lambda n, r=r: combine(1, r, 1 + 2 * (n // 2), lax.rem(n, 2)))
    run(a_back, 'near', 'add')
    run(a_back, 'forward')
    for r in PARTS:
        pl.loop(0, 2)(lambda h, r=r: combine(1, r, 0, h))
    run(a_back, 'arrive')
    for c in range(0, x.shape[1], 128):
        total = x[:, c:c + 128].astype(jnp.float32)
        for r in PARTS:
            if SPAN_STARTS[r] <= c < SPAN_STARTS[r] + SPAN:
                cut = slice(c - SPAN_STARTS[r], c - SPAN_STARTS[r] + 128)
                total += sums[r][place.coord[first[r]], :, cut] + got[r][0, :, cut] + got[r][1, :, cut]
        y[:, c:c + 128] = total.astype(y.dtype)
    run(a_small + a_out + [along_y, along_z, swap] + a_gate + c_out + c_back + b_back + a_back, 'drain')


def solution(mesh):
    dev_axes = ('ep2', 'ep')
    bf16, f32, i32 = jnp.bfloat16, jnp.float32, jnp.int32
    group_size = mesh.shape['ep2'] * mesh.shape['ep']
    anywhere, near, dma = pl.BlockSpec(memory_space=pl.ANY), pl.BlockSpec(memory_space=pltpu.VMEM), pltpu.SemaphoreType.DMA
    vmem = lambda shapes, dtype: [pltpu.VMEM(shape, dtype) for shape in shapes]
    per_part = lambda *lead: [lead + (RING, RING, LANES, WIDTHS[q][r]) for q, r in BOTH]

    def local_step(x, ids, gate, w_a, w_b):
        n_tok, d_model = x.shape
        n_top = ids.shape[1]
        experts = w_a.shape[0] * group_size
        capacity = 8 * ((5 * group_size * n_tok * n_top) // (32 * experts))
        small = (2, n_top, n_tok // 2)
        ids_t, gate_t = ids.T, gate.T
        shape = jax.ShapeDtypeStruct
        slot, counts = pl.pallas_call(route_kernel, out_shape=(shape(small, i32), shape((2, n_top, experts // 2), i32)), name='route')(ids_t)
        between = per_part(RING, 2) * 3 + per_part(2) * 4
        lanes = 4 + 3 + 2 + 1 + 3 + 4 * 6 + 3
        return pl.pallas_call(
            functools.partial(layer_kernel, capacity),
            in_specs=[near] * 5 + [anywhere] * 2,
            out_specs=[near] + [anywhere] * len(between),
            out_shape=[shape(x.shape, x.dtype)] + [shape(s, bf16) for s in between],
            scratch_shapes=vmem([(RING, n_tok, SPAN)] * 3, bf16) + vmem([(RING,) + small] * 3, i32) + vmem([(RING,) + small] * 3, f32)
            + vmem(per_part(RING, 2), bf16) + vmem(per_part(2, RING), bf16) + vmem([(RING, n_tok, SPAN)] * 3, f32)
            + vmem([(2, n_tok, SPAN)] * 3, f32) + vmem([(2, n_tok // 2, SPAN)] * 3, f32)
            + vmem([(RING,) + small, (RING, RING) + small] + [(RING, RING, RING) + small] * 2, i32) + vmem([small], f32)
            + vmem([w_a.shape[1:], w_b.shape[1:]], bf16) + [dma((lanes, 9)), dma((lanes, 9)), dma((lanes, 2)), dma((34,))],
            compiler_params=pltpu.CompilerParams(collective_id=0, has_side_effects=True, vmem_limit_bytes=67043328),
            name='layer',
        )(x, ids_t, gate_t, slot, counts, w_a, w_b)[0]

    tok_spec = P(('dp', 'ep2', 'ep'), None)
    w_spec = P(dev_axes, None, None)
    return jax.shard_map(local_step, mesh=mesh, in_specs=(tok_spec, tok_spec, tok_spec, w_spec, w_spec), out_specs=tok_spec, check_vma=False)
```

time: 362 us -> 329 us (0.909)
  Pallas kernels: 359 us -> 326 us
    pallas_call x4 -> x1, Pallas kernels: 357 us -> 324 us  [local_step(): pl.pallas_call(functools.partial(layer_kernel, capacity), in_specs=[near]...]
where the time goes in v5:
time: 329 us; the launch traced here: 328 us
  Pallas kernels  326 us (99%)
    pallas_call x1, Pallas kernels, local_step(): pl.pallas_call(functools.partial(layer_kernel, capacity), in_specs=[near]...  324 us

profile of v5, /device:TPU:1, one launch (start us, length us, event | category | flops | bytes accessed | tf_op | source)
XLA Modules:
  0.0 328.4 jit_solution(8846649067253970231)
XLA Ops:
  0.0 1.8 route.1
  1.8 324.3 %layer.1 = (bf16[256,2048]{1,0:T(8,128)(2,1)}, bf16[4,2,4,4,16,640]{5,4,3,2,1,0:T(8,128)(2,1)}, bf16[4,2,4,4,16,640]{5,4,3,2,1,0:T(8,128)(2,1)}, bf16[4,2,4,4,16...) custom-call(bf16[256,2048]{1,0:T(8,128)(2,1)} %refs_0_.1, ...), custom_call_target="tpu_custom_call" | custom-call | tf_op jit(solution)/shard_map/layer/pallas_call | solution.py:429
  326.1 2.3 copy.7

commit v6 on v5

--- a/solution.py
+++ b/solution.py
@@ -80,15 +80,21 @@
             k, c, r = (p.core, h, 6 + p.core) if self.switch else (h, p.core, 6 + h)
             self.start(self.relay.at[h], self.target(p.pos(self.axis, -step), k), 6 + h, r, c, p.at(self.axis, step))
 
-    def arrive(self):
+    def arrive_near(self):
         p = self.place
         for d, step in ((0, -1), (1, 1)):
             for k in (0, 1):
                 self.landed(self.target(p.pos(self.axis, step), k), 2 + 2 * d + k)
-        for k in (0, 1):
-            self.landed(self.target(p.pos(self.axis, 2), k), 6 + k)
         if self.switch:
             self.landed(self.target(p.coord[self.axis], p.other), 8)
+
+    def arrive_far(self):
+        for k in (0, 1):
+            self.landed(self.target(self.place.pos(self.axis, 2), k), 6 + k)
+
+    def arrive(self):
+        self.arrive_near()
+        self.arrive_far()
 
     def own(self, local):
         p = self.place
@@ -168,7 +174,7 @@
     return dev * (2 * LANES) + q * LANES + (row & (LANES - 1))
 
 
-def route_kernel(ids_ref, slot_ref, count_ref):
+def route(ids_ref, slot_ref, count_ref):
     ids = ids_ref[...]
     n_top, n_tok = ids.shape
     experts = 2 * count_ref.shape[2]
@@ -194,8 +200,8 @@
 
 
 def layer_kernel(capacity, *refs):
-    (x, ids, gate, slot, count), (w_in, w_out), (y,), mids, backs, ends, b_relay, c_relay, cb_relay, bb_relay, refs = take(refs, 5, 2, 1, 6, 6, 6, 6, 6, 6, 6, None)
-    tokens, slots, gates, packed, rows, sums, got, sum_relay, (count_x, count_y, count_z, count_other, mine, w_in_v, w_out_v, send, recv, local, extra) = take(refs, 3, 3, 3, 6, 6, 3, 3, 3, None)
+    (x, ids, gate), (w_in, w_out), (y,), mids, backs, ends, b_relay, c_relay, cb_relay, bb_relay, refs = take(refs, 3, 2, 1, 6, 6, 6, 6, 6, 6, 6, None)
+    tokens, slots, gates, packed, rows, sums, got, sum_relay, (slot, count, count_x, count_y, count_z, count_other, mine, w_in_v, w_out_v, send, recv, local, extra) = take(refs, 3, 3, 3, 6, 6, 3, 3, 3, None)
     place = Place()
     n_tok, n_top = x.shape[0], slot.shape[1]
     half = n_tok // 2
@@ -251,8 +257,8 @@
             rows[3 * q + r][core, z] = res.astype(jnp.bfloat16).reshape(RING, RING, LANES, WIDTHS[q][r])
 
     def weigh():
-        counted = lambda ref: ref[...].reshape((RING**3,) + count.shape)
-        ahead = lax.broadcasted_iota(jnp.int32, (RING**3,) + count.shape, 0) < place.chip
+        counted = lambda ref: ref[...].reshape((RING**3,) + slot.shape)
+        ahead = lax.broadcasted_iota(jnp.int32, (RING**3,) + slot.shape, 0) < place.chip
         off = jnp.sum(jnp.where(ahead, counted(count_z), 0), axis=0) + jnp.where(place.core == 1, jnp.sum(counted(count_other), axis=0), 0)
         off = jnp.concatenate([off[0], off[1]], axis=1)
         high, low = (off >> 7).astype(jnp.bfloat16), (off & 127).astype(jnp.bfloat16)
@@ -266,10 +272,11 @@
                 rank = before[:, cut] + slot[h, j:j + 1] - ids[j:j + 1, cut] * LANES
                 mine[h, j:j + 1] = jnp.where(rank < capacity, gate[j:j + 1, cut], 0.0)
 
-    def combine(q, r, step, h):
+    def combine(q, r, step, h, b=None):
         a = place.pos(first[r], step)
-        wanted = plane_slots((n_row, half), ORDERS[r], place, q)
-        weight = jnp.zeros((n_row, half), jnp.float32)
+        lead, n = (slice(None), n_row) if b is None else (pl.ds(b, 1), n_row // RING)
+        wanted = plane_slots((n, half), ORDERS[r], place, q, 0 if b is None else b * n)
+        weight = jnp.zeros((n, half), jnp.float32)
         for j in range(n_top):
             weight = jnp.where(wanted == slots[r][a, h, j:j + 1], gates[r][a, h, j:j + 1], weight)
         high = weight.astype(jnp.bfloat16)
@@ -279,7 +286,7 @@
         weights = jnp.concatenate([high, mid, low], axis=1)
         offset = STARTS[q][r] - SPAN_STARTS[r]
         for lo, hi in ((0, 384), (384, WIDTHS[q][r])):
-            back = packed[3 * q + r][:, :, :, a, :, lo:hi].reshape(n_row, hi - lo)
+            back = packed[3 * q + r][lead, :, :, a, :, lo:hi].reshape(n, hi - lo)
             mix = lax.dot_general(weights, back, (((0,), (0,)), ((), ())), preferred_element_type=jnp.float32)
             sums[r][a, pl.ds(pl.multiple_of(h * half, half), half), offset + lo:offset + hi] += mix[:half] + mix[half:2 * half] + mix[2 * half:]
 
@@ -299,25 +306,29 @@
         me = [place.coord[item.axis] for item in lanes]
         return [load(item.source(me[r], place.core), packed[i + r].at[me[r], place.core], 4 + i + r) for r, item in enumerate(lanes)]
 
-    def fetch(i):
+    def fetch(i, near):
         axis = second[i % 3]
-        pieces = [(place.pos(axis, step),) for step in (1, 2, 3)] + [(place.coord[axis], place.other)]
-        return [load(ends[i].at[at], packed[i].at[at], 10 + 4 * i + n) for n, at in enumerate(pieces)]
-
-    kept = own(a_small + a_out)
+        pieces = [(place.pos(axis, step),) for step in ((1, 3) if near else (2,))]
+        if near:
+            pieces.append((place.coord[axis], place.other))
+        return [load(ends[i].at[at], packed[i].at[at], 10 + 4 * i + n + (0 if near else 3)) for n, at in enumerate(pieces)]
+
+    kept = own(a_out)
     weights = [load(w_in.at[0], w_in_v, 0), load(w_out.at[0], w_out_v, 1)]
     place.greet(True)
+    run(a_out, 'near')
+    route(ids, slot, count)
+    kept += own(a_small)
     run(a_small, 'near')
-    run(a_out, 'near')
     wait(kept)
     for r in PARTS:
         pack(0, r, 0)
-    run(a_small, 'forward')
     run(a_out, 'forward')
-    run(a_small, 'arrive_near', 'arrive_far')
+    run(a_small, 'forward', 'arrive_near')
     run(a_out, 'arrive_near')
     for r in PARTS:
         pl.loop(0, 2)(lambda n, r=r: pack(0, r, 1 + 2 * n))
+    run(a_small, 'arrive_far')
     run(a_out, 'arrive_far')
     for r in PARTS:
         pack(0, r, 2)
@@ -330,18 +341,16 @@
     run(b_out[one], 'forward')
     run(b_out[two], 'far', 'near')
     kept_b += own(b_out[two])
-    run([along_y], 'forward', 'arrive_near', 'arrive_far')
+    run([along_y], 'forward')
+    run(b_out[two], 'forward')
+    wait(kept_b)
+    run(b_out[one], 'arrive')
+    run(c_out[one], 'far', 'near')
+    kept = own(c_out[one])
+    run([along_y], 'arrive_near', 'arrive_far')
     wait(kept_y)
     kept_z = own([along_z])
     run([along_z], 'near')
-    wait(kept_b)
-    run(b_out[two], 'forward')
-    run(b_out[one], 'arrive')
-    run(c_out[one], 'far', 'near')
-    kept = own(c_out[one])
-    run([along_z], 'forward', 'arrive_near', 'arrive_far')
-    wait(kept_z)
-    swap.start(count_z, count_other, 0, 0, place.other, place.chip)
     run(c_out[one], 'forward')
     run(b_out[two], 'arrive')
     run(c_out[two], 'far', 'near')
@@ -353,56 +362,70 @@
     run(c_out[two], 'forward')
     run(c_back[one], 'far', 'near')
     kept = own(c_back[one])
+    run([along_z], 'forward')
     run(c_out[two], 'arrive')
     wait(kept_two + weights)
     pl.loop(0, 2 * RING)(lambda n: expert(1, n))
     run(c_back[one], 'forward')
     run(c_back[two], 'far', 'near')
     kept_two = own(c_back[two])
+    run([along_z], 'arrive_near', 'arrive_far')
+    wait(kept_z)
+    swap.start(count_z, count_other, 0, 0, place.other, place.chip)
     swap.landed(count_other, 0)
     weigh()
-    wait(kept)
+    kept_gate = own(a_gate)
+    run(a_gate, 'near')
     run(c_back[two], 'forward')
     run(c_back[one], 'arrive')
+    wait(kept)
     run(b_back[one], 'far', 'near')
     run(b_out, 'drain')
     kept = own_rows(b_back[one], 0)
-    kept_gate = own(a_gate)
-    run(a_gate, 'near')
     for r in PARTS:
         sums[r][...] = jnp.zeros_like(sums[r])
-    run(a_gate, 'forward', 'arrive_near', 'arrive_far')
-    wait(kept_gate + kept_two)
+    run(a_gate, 'forward')
     run(b_back[one], 'forward')
     run(c_back[two], 'arrive')
+    wait(kept_two)
     run(b_back[two], 'far', 'near')
     kept_two = own_rows(b_back[two], 3)
     run(b_back[one], 'arrive')
     wait(kept)
-    loads = [fetch(r) for r in PARTS]
+    loads = [fetch(r, True) + fetch(r, False) for r in PARTS]
+    run(a_gate, 'arrive_near', 'arrive_far')
+    wait(kept_gate)
     for r in PARTS:
         wait(loads[r])
         pl.loop(0, 2 * RING)(lambda n, r=r: combine(0, r, n // 2, lax.rem(n, 2)))
-    run(b_back[two], 'forward', 'arrive')
+    run(b_back[two], 'forward', 'arrive_near')
+    loads = [fetch(3 + r, True) for r in PARTS]
     wait(kept_two)
-    loads = [fetch(3 + r) for r in PARTS]
     for r in PARTS:
         wait(loads[r])
-        pl.loop(0, 2)(lambda h, r=r: combine(1, r, 2, h))
+        pl.loop(0, 6 * RING)(lambda n, r=r: combine(1, r, n // 6, lax.rem(n, 2), place.pos(second[r], 3 + lax.rem(n, 6) // 2)))
+    run(b_back[two], 'arrive_far')
+    loads = [fetch(3 + r, False) for r in PARTS]
+    for r in PARTS:
+        wait(loads[r])
+        pl.loop(0, 2)(lambda h, r=r: combine(1, r, 2, h, place.pos(second[r], 2)))
     run(a_back, 'far')
     for r in PARTS:
-        pl.loop(0, 4)(lambda n, r=r: combine(1, r, 1 + 2 * (n // 2), lax.rem(n, 2)))
+        pl.loop(0, 4)(lambda n, r=r: combine(1, r, 1 + 2 * (n // 2), lax.rem(n, 2), place.pos(second[r], 2)))
     run(a_back, 'near', 'add')
     run(a_back, 'forward')
     for r in PARTS:
-        pl.loop(0, 2)(lambda h, r=r: combine(1, r, 0, h))
+        pl.loop(0, 2)(lambda h, r=r: combine(1, r, 0, h, place.pos(second[r], 2)))
+        sums[r][place.coord[first[r]], :, :SPAN_STARTS[1]] += x[:, SPAN_STARTS[r]:SPAN_STARTS[r] + SPAN_STARTS[1]].astype(jnp.float32)
+    sums[2][place.coord[first[2]], :, SPAN_STARTS[1]:] += x[:, SPAN_STARTS[2] + SPAN_STARTS[1]:].astype(jnp.float32)
     run(a_back, 'arrive')
     for c in range(0, x.shape[1], 128):
-        total = x[:, c:c + 128].astype(jnp.float32)
+        total = None
         for r in PARTS:
             if SPAN_STARTS[r] <= c < SPAN_STARTS[r] + SPAN:
                 cut = slice(c - SPAN_STARTS[r], c - SPAN_STARTS[r] + 128)
-                total += sums[r][place.coord[first[r]], :, cut] + got[r][0, :, cut] + got[r][1, :, cut]
+                part = sums[r][place.coord[first[r]], :, cut] + got[r][0, :, cut] + got[r][1, :, cut]
+                total = part if total is None else total + part
         y[:, c:c + 128] = total.astype(y.dtype)
     run(a_small + a_out + [along_y, along_z, swap] + a_gate + c_out + c_back + b_back + a_back, 'drain')
 
@@ -423,22 +446,21 @@
         small = (2, n_top, n_tok // 2)
         ids_t, gate_t = ids.T, gate.T
         shape = jax.ShapeDtypeStruct
-        slot, counts = pl.pallas_call(route_kernel, out_shape=(shape(small, i32), shape((2, n_top, experts // 2), i32)), name='route')(ids_t)
         between = per_part(RING, 2) * 3 + per_part(2) * 4
         lanes = 4 + 3 + 2 + 1 + 3 + 4 * 6 + 3
         return pl.pallas_call(
             functools.partial(layer_kernel, capacity),
-            in_specs=[near] * 5 + [anywhere] * 2,
+            in_specs=[near] * 3 + [anywhere] * 2,
             out_specs=[near] + [anywhere] * len(between),
             out_shape=[shape(x.shape, x.dtype)] + [shape(s, bf16) for s in between],
             scratch_shapes=vmem([(RING, n_tok, SPAN)] * 3, bf16) + vmem([(RING,) + small] * 3, i32) + vmem([(RING,) + small] * 3, f32)
             + vmem(per_part(RING, 2), bf16) + vmem(per_part(2, RING), bf16) + vmem([(RING, n_tok, SPAN)] * 3, f32)
             + vmem([(2, n_tok, SPAN)] * 3, f32) + vmem([(2, n_tok // 2, SPAN)] * 3, f32)
-            + vmem([(RING,) + small, (RING, RING) + small] + [(RING, RING, RING) + small] * 2, i32) + vmem([small], f32)
+            + vmem([small, (2, n_top, experts // 2), (RING,) + small, (RING, RING) + small] + [(RING, RING, RING) + small] * 2, i32) + vmem([small], f32)
             + vmem([w_a.shape[1:], w_b.shape[1:]], bf16) + [dma((lanes, 9)), dma((lanes, 9)), dma((lanes, 2)), dma((34,))],
             compiler_params=pltpu.CompilerParams(collective_id=0, has_side_effects=True, vmem_limit_bytes=67043328),
             name='layer',
-        )(x, ids_t, gate_t, slot, counts, w_a, w_b)[0]
+        )(x, ids_t, gate_t, w_a, w_b)[0]
 
     tok_spec = P(('dp', 'ep2', 'ep'), None)
     w_spec = P(dev_axes, None, None)

time: 329 us -> 338 us (1.027)
  Pallas kernels: 326 us -> 335 us
    pallas_call x1, Pallas kernels: 324 us -> 335 us  [local_step(): pl.pallas_call(functools.partial(layer_kernel, capacity), in_specs=[near]...]
where the time goes in v6:
time: 338 us; the launch traced here: 337 us
  Pallas kernels  335 us (99%)
    pallas_call x1, Pallas kernels, local_step(): pl.pallas_call(functools.partial(layer_kernel, capacity), in_specs=[near]...  335 us

profile of v6, /device:TPU:1, one launch (start us, length us, event | category | flops | bytes accessed | tf_op | source)
XLA Modules:
  0.0 337.5 jit_solution(7854553648962890593)
XLA Ops:
  0.0 335.2 %layer.1 = (bf16[256,2048]{1,0:T(8,128)(2,1)}, bf16[4,2,4,4,16,640]{5,4,3,2,1,0:T(8,128)(2,1)}, bf16[4,2,4,4,16,640]{5,4,3,2,1,0:T(8,128)(2,1)}, bf16[4,2,4,4,16...) custom-call(bf16[256,2048]{1,0:T(8,128)(2,1)} %refs_0_.1, ...), custom_call_target="tpu_custom_call" | custom-call | tf_op jit(solution)/shard_map/layer/pallas_call | solution.py:451
  335.2 2.3 copy.7

commit v7 on v6

--- a/solution.py
+++ b/solution.py
@@ -272,11 +272,10 @@
                 rank = before[:, cut] + slot[h, j:j + 1] - ids[j:j + 1, cut] * LANES
                 mine[h, j:j + 1] = jnp.where(rank < capacity, gate[j:j + 1, cut], 0.0)
 
-    def combine(q, r, step, h, b=None):
+    def combine(q, r, step, h):
         a = place.pos(first[r], step)
-        lead, n = (slice(None), n_row) if b is None else (pl.ds(b, 1), n_row // RING)
-        wanted = plane_slots((n, half), ORDERS[r], place, q, 0 if b is None else b * n)
-        weight = jnp.zeros((n, half), jnp.float32)
+        wanted = plane_slots((n_row, half), ORDERS[r], place, q)
+        weight = jnp.zeros((n_row, half), jnp.float32)
         for j in range(n_top):
             weight = jnp.where(wanted == slots[r][a, h, j:j + 1], gates[r][a, h, j:j + 1], weight)
         high = weight.astype(jnp.bfloat16)
@@ -286,7 +285,7 @@
         weights = jnp.concatenate([high, mid, low], axis=1)
         offset = STARTS[q][r] - SPAN_STARTS[r]
         for lo, hi in ((0, 384), (384, WIDTHS[q][r])):
-            back = packed[3 * q + r][lead, :, :, a, :, lo:hi].reshape(n, hi - lo)
+            back = packed[3 * q + r][:, :, :, a, :, lo:hi].reshape(n_row, hi - lo)
             mix = lax.dot_general(weights, back, (((0,), (0,)), ((), ())), preferred_element_type=jnp.float32)
             sums[r][a, pl.ds(pl.multiple_of(h * half, half), half), offset + lo:offset + hi] += mix[:half] + mix[half:2 * half] + mix[2 * half:]
 
@@ -401,21 +400,18 @@
     run(b_back[two], 'forward', 'arrive_near')
     loads = [fetch(3 + r, True) for r in PARTS]
     wait(kept_two)
+    run(b_back[two], 'arrive_far')
+    loads = [loads[r] + fetch(3 + r, False) for r in PARTS]
     for r in PARTS:
         wait(loads[r])
-        pl.loop(0, 6 * RING)(lambda n, r=r: combine(1, r, n // 6, lax.rem(n, 2), place.pos(second[r], 3 + lax.rem(n, 6) // 2)))
-    run(b_back[two], 'arrive_far')
-    loads = [fetch(3 + r, False) for r in PARTS]
-    for r in PARTS:
-        wait(loads[r])
-        pl.loop(0, 2)(lambda h, r=r: combine(1, r, 2, h, place.pos(second[r], 2)))
+        pl.loop(0, 2)(lambda h, r=r: combine(1, r, 2, h))
     run(a_back, 'far')
     for r in PARTS:
-        pl.loop(0, 4)(lambda n, r=r: combine(1, r, 1 + 2 * (n // 2), lax.rem(n, 2), place.pos(second[r], 2)))
+        pl.loop(0, 4)(lambda n, r=r: combine(1, r, 1 + 2 * (n // 2), lax.rem(n, 2)))
     run(a_back, 'near', 'add')
     run(a_back, 'forward')
     for r in PARTS:
-        pl.loop(0, 2)(lambda h, r=r: combine(1, r, 0, h, place.pos(second[r], 2)))
+        pl.loop(0, 2)(lambda h, r=r: combine(1, r, 0, h))
         sums[r][place.coord[first[r]], :, :SPAN_STARTS[1]] += x[:, SPAN_STARTS[r]:SPAN_STARTS[r] + SPAN_STARTS[1]].astype(jnp.float32)
     sums[2][place.coord[first[2]], :, SPAN_STARTS[1]:] += x[:, SPAN_STARTS[2] + SPAN_STARTS[1]:].astype(jnp.float32)
     run(a_back, 'arrive')

time: 338 us -> 320 us (0.947)
  Pallas kernels: 335 us -> 317 us
    pallas_call x1, Pallas kernels: 335 us -> 317 us  [local_step(): pl.pallas_call(functools.partial(layer_kernel, capacity), in_specs=[near]...]
where the time goes in v7:
time: 320 us
  Pallas kernels  317 us (99%)
    pallas_call x1, Pallas kernels, local_step(): pl.pallas_call(functools.partial(layer_kernel, capacity), in_specs=[near]...  317 us

profile of v7, /device:TPU:1, one launch (start us, length us, event | category | flops | bytes accessed | tf_op | source)
XLA Modules:
  0.0 319.7 jit_solution(12811472748280416917)
XLA Ops:
  0.0 317.4 %layer.1 = (bf16[256,2048]{1,0:T(8,128)(2,1)}, bf16[4,2,4,4,16,640]{5,4,3,2,1,0:T(8,128)(2,1)}, bf16[4,2,4,4,16,640]{5,4,3,2,1,0:T(8,128)(2,1)}, bf16[4,2,4,4,16...) custom-call(bf16[256,2048]{1,0:T(8,128)(2,1)} %refs_0_.1, ...), custom_call_target="tpu_custom_call" | custom-call | tf_op jit(solution)/shard_map/layer/pallas_call | solution.py:447
  317.4 2.3 copy.7

commit v8 on v7

--- a/solution.py
+++ b/solution.py
@@ -111,6 +111,13 @@
 
 
 class Gather(Lane):
+    def near(self):
+        p = self.place
+        me = p.coord[self.axis]
+        for d, step, halves in ((0, 1, (0, 1)), (1, -1, (1, 0))):
+            for h in halves:
+                self.start(self.source(me, h), self.target(me, h), 2 + 2 * d + h, 2 + 2 * d + h, p.core, p.at(self.axis, step))
+
     def forward(self):
         p = self.place
         for h, step in ((0, 1), (1, -1)):
@@ -171,6 +178,13 @@
     row = lax.broadcasted_iota(jnp.int32, shape, 0) + base
     first, second, third = [STRIDE[axis] for axis in order]
     dev = ((row >> 6) & 1) * RING**3 + (row >> 7) * second + ((row >> 4) & (RING - 1)) * third + place.coord[order[0]] * first
+    return dev * (2 * LANES) + q * LANES + (row & (LANES - 1))
+
+
+def line_slots(shape, order, place, q):
+    row = lax.broadcasted_iota(jnp.int32, shape, 0)
+    first, second, third = [STRIDE[axis] for axis in order]
+    dev = ((row >> 4) & 1) * RING**3 + (row >> 5) * third + place.coord[order[0]] * first + place.coord[order[1]] * second
     return dev * (2 * LANES) + q * LANES + (row & (LANES - 1))
 
 
@@ -200,8 +214,8 @@
 
 
 def layer_kernel(capacity, *refs):
-    (x, ids, gate), (w_in, w_out), (y,), mids, backs, ends, b_relay, c_relay, cb_relay, bb_relay, refs = take(refs, 3, 2, 1, 6, 6, 6, 6, 6, 6, 6, None)
-    tokens, slots, gates, packed, rows, sums, got, sum_relay, (slot, count, count_x, count_y, count_z, count_other, mine, w_in_v, w_out_v, send, recv, local, extra) = take(refs, 3, 3, 3, 6, 6, 3, 3, 3, None)
+    (x, ids, gate), (w_in, w_out), (y,), wide, backs, ends, c_relay, cb_relay, bb_relay, refs = take(refs, 3, 2, 1, 3, 6, 6, 6, 6, 6, None)
+    tokens, slots, wide_slots, gates, packed, rows, sums, got, sum_relay, (slot, count, count_x, count_y, count_z, count_other, mine, w_in_v, w_out_v, send, recv, local, extra) = take(refs, 3, 3, 3, 3, 6, 6, 3, 3, 3, None)
     place = Place()
     n_tok, n_top = x.shape[0], slot.shape[1]
     half = n_tok // 2
@@ -218,10 +232,10 @@
     along_z = lane(Gather, 'z', lambda p, h: count_y.at[:, :, h], lambda o, k: count_z.at[o, :, :, k])
     swap = lane(Lane, 'z', None, None)
     a_gate = [lane(Gather, first[r], lambda p, h: mine.at[h], lambda o, k, r=r: gates[r].at[o, k]) for r in PARTS]
-    b_out = [lane(Lane, second[r], lambda p, h, i=3 * q + r: packed[i].at[p, h],
-                  lambda o, k, i=3 * q + r, r=r: mids[i].at[(slice(None), k) + spot(second[r], ORDERS[r][:2], o)], b_relay[3 * q + r], True) for q, r in BOTH]
-    c_out = [lane(Lane, third[r], lambda p, h, i=3 * q + r: mids[i].at[p, h],
-                  lambda o, k, i=3 * q + r, r=r: rows[i].at[(k,) + spot(third[r], 'zyx', o)], c_relay[3 * q + r]) for q, r in BOTH]
+    b_small = [lane(Gather, second[r], lambda p, h, r=r: slots[r].at[pl.ds(2 * h, 2)], lambda o, k, r=r: wide_slots[r].at[o, pl.ds(2 * k, 2)]) for r in PARTS]
+    b_out = [lane(Gather, second[r], lambda p, h, r=r: tokens[r].at[pl.ds(2 * h, 2)], lambda o, k, r=r: wide[r].at[o, pl.ds(2 * k, 2)]) for r in PARTS]
+    c_out = [lane(Lane, third[r], lambda p, h, i=3 * q + r: packed[i].at[p, h],
+                  lambda o, k, i=3 * q + r, r=r: rows[i].at[(k,) + spot(third[r], 'zyx', o)], c_relay[3 * q + r], True) for q, r in BOTH]
     c_back = [lane(Lane, third[r], lambda p, h, i=3 * q + r, r=r: rows[i].at[(h,) + spot(third[r], 'zyx', p)],
                    lambda o, k, i=3 * q + r: backs[i].at[o, k], cb_relay[3 * q + r]) for q, r in BOTH]
     b_back = [lane(Lane, second[r], lambda p, h, i=3 * q + r, r=r: backs[i].at[(slice(None), h) + spot(second[r], ORDERS[r][:2], p)],
@@ -230,19 +244,20 @@
                    lambda side, h, r=r: got[r].at[side, pl.ds(h * half, half)], sum_relay[r]) for r in PARTS]
     one, two = slice(0, 3), slice(3, 6)
 
-    def pack(q, r, step):
-        a = place.pos(first[r], step)
+    def pack(q, r, step, a):
+        b = place.pos(second[r], step)
+        n = 2 * RING * LANES
+        wanted = line_slots((n, half), ORDERS[r], place, q)
+        picks = []
+        for h in (0, 1):
+            pick = jnp.zeros((n, half), jnp.float32)
+            for j in range(n_top):
+                pick = jnp.where(wanted == wide_slots[r][b, a, h, j:j + 1], 1.0, pick)
+            picks.append(pick.astype(jnp.bfloat16))
         offset = STARTS[q][r] - SPAN_STARTS[r]
-        for part in (0, 1):
-            wanted = plane_slots((n_row // 2, half), ORDERS[r], place, q, part * n_row // 2)
-            picks = []
-            for h in (0, 1):
-                pick = jnp.zeros((n_row // 2, half), jnp.float32)
-                for j in range(n_top):
-                    pick = jnp.where(wanted == slots[r][a, h, j:j + 1], 1.0, pick)
-                picks.append(pick.astype(jnp.bfloat16))
-            block = jnp.dot(jnp.concatenate(picks, axis=1), tokens[r][a, :, offset:offset + WIDTHS[q][r]], preferred_element_type=jnp.float32)
-            packed[3 * q + r][2 * part:2 * part + 2, :, :, a] = block.astype(jnp.bfloat16).reshape(RING // 2, 2, RING, LANES, WIDTHS[q][r])
+        block = jnp.dot(jnp.concatenate(picks, axis=1), tokens[r][a, :, offset:offset + WIDTHS[q][r]], preferred_element_type=jnp.float32)
+        spots = (b, a) if 'zyx'.index(second[r]) < 'zyx'.index(first[r]) else (a, b)
+        packed[3 * q + r][(slice(None), slice(None)) + spots] = block.astype(jnp.bfloat16).reshape(RING, 2, LANES, WIDTHS[q][r])
 
     def expert(q, step):
         core, z = step // RING, lax.rem(step, RING)
@@ -293,6 +308,11 @@
         for copy in copies:
             copy.wait()
 
+    def wait_sent(item, count):
+        for copy in item.sent[:count]:
+            copy.wait_send()
+        del item.sent[:count]
+
     def own(lanes):
         return [copy for item in lanes for copy in item.own(local)]
 
@@ -311,6 +331,9 @@
         if near:
             pieces.append((place.coord[axis], place.other))
         return [load(ends[i].at[at], packed[i].at[at], 10 + 4 * i + n + (0 if near else 3)) for n, at in enumerate(pieces)]
+
+    def slabs(step):
+        return [load(wide[r].at[place.pos(second[r], step)], tokens[r], 4 + r) for r in PARTS]
 
     kept = own(a_out)
     weights = [load(w_in.at[0], w_in_v, 0), load(w_out.at[0], w_out_v, 1)]
@@ -320,40 +343,47 @@
     kept += own(a_small)
     run(a_small, 'near')
     wait(kept)
-    for r in PARTS:
-        pack(0, r, 0)
     run(a_out, 'forward')
-    run(a_small, 'forward', 'arrive_near')
-    run(a_out, 'arrive_near')
-    for r in PARTS:
-        pl.loop(0, 2)(lambda n, r=r: pack(0, r, 1 + 2 * n))
-    run(a_small, 'arrive_far')
-    run(a_out, 'arrive_far')
-    for r in PARTS:
-        pack(0, r, 2)
-    run(b_out[one], 'far', 'near')
-    kept_y = own([along_y])
-    run([along_y], 'near')
-    kept_b = own(b_out[one])
-    for r in PARTS:
-        pl.loop(0, RING)(lambda n, r=r: pack(1, r, n))
-    run(b_out[one], 'forward')
-    run(b_out[two], 'far', 'near')
-    kept_b += own(b_out[two])
-    run([along_y], 'forward')
-    run(b_out[two], 'forward')
-    wait(kept_b)
-    run(b_out[one], 'arrive')
+    run(a_small, 'forward', 'arrive_near', 'arrive_far')
+    kept = own(b_small + [along_y])
+    run(b_small + [along_y], 'near')
+    run(a_out, 'arrive_near', 'arrive_far')
+    run(b_out, 'near')
+    run(b_small + [along_y], 'forward')
+    wait(kept)
+    for r in PARTS:
+        pl.loop(0, RING)(lambda a, r=r: [pack(q, r, 0, a) for q in STREAMS] and None)
+    run(b_out, 'forward')
+    run(b_small, 'arrive_near')
+    run(b_out, 'arrive_near')
+    run(a_out, 'drain')
+    for item in b_out:
+        wait_sent(item, 4)
+
+    @pl.loop(0, 2)
+    def _(n):
+        loads = slabs(1 + 2 * n)
+        for r in PARTS:
+            loads[r].wait()
+            pl.loop(0, RING)(lambda a, r=r: [pack(q, r, 1 + 2 * n, a) for q in STREAMS] and None)
+
+    run(b_small + [along_y], 'arrive_far')
+    run([along_y], 'arrive_near')
+    kept_z = own([along_z])
+    run([along_z], 'near')
+    run(b_out, 'arrive_far')
+    loads = slabs(2)
+    for r in PARTS:
+        loads[r].wait()
+        pl.loop(0, RING)(lambda a, r=r: pack(0, r, 2, a))
     run(c_out[one], 'far', 'near')
     kept = own(c_out[one])
-    run([along_y], 'arrive_near', 'arrive_far')
-    wait(kept_y)
-    kept_z = own([along_z])
-    run([along_z], 'near')
+    for r in PARTS:
+        pl.loop(0, RING)(lambda a, r=r: pack(1, r, 2, a))
     run(c_out[one], 'forward')
-    run(b_out[two], 'arrive')
     run(c_out[two], 'far', 'near')
     kept_two = own(c_out[two])
+    run([along_z], 'forward')
     run(c_out[one], 'arrive')
     wait(kept + weights)
     pl.loop(0, 2 * RING)(lambda n: expert(0, n))
@@ -361,7 +391,6 @@
     run(c_out[two], 'forward')
     run(c_back[one], 'far', 'near')
     kept = own(c_back[one])
-    run([along_z], 'forward')
     run(c_out[two], 'arrive')
     wait(kept_two + weights)
     pl.loop(0, 2 * RING)(lambda n: expert(1, n))
@@ -379,7 +408,7 @@
     run(c_back[one], 'arrive')
     wait(kept)
     run(b_back[one], 'far', 'near')
-    run(b_out, 'drain')
+    run(c_out, 'drain')
     kept = own_rows(b_back[one], 0)
     for r in PARTS:
         sums[r][...] = jnp.zeros_like(sums[r])
@@ -423,7 +452,7 @@
                 part = sums[r][place.coord[first[r]], :, cut] + got[r][0, :, cut] + got[r][1, :, cut]
                 total = part if total is None else total + part
         y[:, c:c + 128] = total.astype(y.dtype)
-    run(a_small + a_out + [along_y, along_z, swap] + a_gate + c_out + c_back + b_back + a_back, 'drain')
+    run(a_small + b_small + b_out + [along_y, along_z, swap] + a_gate + c_back + b_back + a_back, 'drain')
 
 
 def solution(mesh):
@@ -442,14 +471,14 @@
         small = (2, n_top, n_tok // 2)
         ids_t, gate_t = ids.T, gate.T
         shape = jax.ShapeDtypeStruct
-        between = per_part(RING, 2) * 3 + per_part(2) * 4
-        lanes = 4 + 3 + 2 + 1 + 3 + 4 * 6 + 3
+        between = [(RING, RING, n_tok, SPAN)] * 3 + per_part(RING, 2) * 2 + per_part(2) * 3
+        lanes = 4 + 3 + 2 + 1 + 3 + 3 + 3 + 3 * 6 + 3
         return pl.pallas_call(
             functools.partial(layer_kernel, capacity),
             in_specs=[near] * 3 + [anywhere] * 2,
             out_specs=[near] + [anywhere] * len(between),
             out_shape=[shape(x.shape, x.dtype)] + [shape(s, bf16) for s in between],
-            scratch_shapes=vmem([(RING, n_tok, SPAN)] * 3, bf16) + vmem([(RING,) + small] * 3, i32) + vmem([(RING,) + small] * 3, f32)
+            scratch_shapes=vmem([(RING, n_tok, SPAN)] * 3, bf16) + vmem([(RING,) + small] * 3 + [(RING, RING) + small] * 3, i32) + vmem([(RING,) + small] * 3, f32)
             + vmem(per_part(RING, 2), bf16) + vmem(per_part(2, RING), bf16) + vmem([(RING, n_tok, SPAN)] * 3, f32)
             + vmem([(2, n_tok, SPAN)] * 3, f32) + vmem([(2, n_tok // 2, SPAN)] * 3, f32)
             + vmem([small, (2, n_top, experts // 2), (RING,) + small, (RING, RING) + small] + [(RING, RING, RING) + small] * 2, i32) + vmem([small], f32)

time: 320 us -> 315 us (0.984)
  Pallas kernels: 317 us -> 313 us
    pallas_call x1, Pallas kernels: 317 us -> 313 us  [local_step(): pl.pallas_call(functools.partial(layer_kernel, capacity), in_specs=[near]...]
where the time goes in v8:
time: 315 us
  Pallas kernels  313 us (99%)
    pallas_call x1, Pallas kernels, local_step(): pl.pallas_call(functools.partial(layer_kernel, capacity), in_specs=[near]...  313 us

profile of v8, /device:TPU:1, one launch (start us, length us, event | category | flops | bytes accessed | tf_op | source)
XLA Modules:
  0.0 314.9 jit_solution(5853701252753804890)
XLA Ops:
  0.0 312.6 %layer.1 = (bf16[256,2048]{1,0:T(8,128)(2,1)}, bf16[4,4,256,768]{3,2,1,0:T(8,128)(2,1)}, bf16[4,4,256,768]{3,2,1,0:T(8,128)(2,1)}, bf16[4,4,256,768]{3,2,1,0:T(8...) custom-call(bf16[256,2048]{1,0:T(8,128)(2,1)} %refs_0_.1, ...), custom_call_target="tpu_custom_call" | custom-call | tf_op jit(solution)/shard_map/layer/pallas_call | solution.py:476
  312.6 2.3 copy.7

commit v9 on v8

--- a/solution.py
+++ b/solution.py
@@ -233,7 +233,9 @@
     swap = lane(Lane, 'z', None, None)
     a_gate = [lane(Gather, first[r], lambda p, h: mine.at[h], lambda o, k, r=r: gates[r].at[o, k]) for r in PARTS]
     b_small = [lane(Gather, second[r], lambda p, h, r=r: slots[r].at[pl.ds(2 * h, 2)], lambda o, k, r=r: wide_slots[r].at[o, pl.ds(2 * k, 2)]) for r in PARTS]
-    b_out = [lane(Gather, second[r], lambda p, h, r=r: tokens[r].at[pl.ds(2 * h, 2)], lambda o, k, r=r: wide[r].at[o, pl.ds(2 * k, 2)]) for r in PARTS]
+    b_out = [lane(Gather, second[r], lambda p, h, r=r, step=step: tokens[r].at[place.pos(first[r], step), pl.ds(h * half, half)],
+                  lambda o, k, r=r, step=step: wide[r].at[o, place.pos(first[r], step), pl.ds(k * half, half)]) for step in (0, 1, 3, 2) for r in PARTS]
+    b_own, b_near, b_far = b_out[:3], b_out[3:9], b_out[9:]
     c_out = [lane(Lane, third[r], lambda p, h, i=3 * q + r: packed[i].at[p, h],
                   lambda o, k, i=3 * q + r, r=r: rows[i].at[(k,) + spot(third[r], 'zyx', o)], c_relay[3 * q + r], True) for q, r in BOTH]
     c_back = [lane(Lane, third[r], lambda p, h, i=3 * q + r, r=r: rows[i].at[(h,) + spot(third[r], 'zyx', p)],
@@ -337,24 +339,30 @@
 
     kept = own(a_out)
     weights = [load(w_in.at[0], w_in_v, 0), load(w_out.at[0], w_out_v, 1)]
-    place.greet(True)
-    run(a_out, 'near')
     route(ids, slot, count)
     kept += own(a_small)
+    place.greet(True)
     run(a_small, 'near')
+    run(a_out, 'near')
+    run(a_small, 'forward')
     wait(kept)
+    run(b_own, 'near')
     run(a_out, 'forward')
-    run(a_small, 'forward', 'arrive_near', 'arrive_far')
+    run(a_small, 'arrive_near', 'arrive_far')
     kept = own(b_small + [along_y])
     run(b_small + [along_y], 'near')
-    run(a_out, 'arrive_near', 'arrive_far')
-    run(b_out, 'near')
+    run(a_out, 'arrive_near')
+    run(b_near, 'near')
+    run(b_own, 'forward')
+    run(a_out, 'arrive_far')
+    run(b_far, 'near')
     run(b_small + [along_y], 'forward')
     wait(kept)
     for r in PARTS:
         pl.loop(0, RING)(lambda a, r=r: [pack(q, r, 0, a) for q in STREAMS] and None)
-    run(b_out, 'forward')
+    run(b_near, 'forward')
     run(b_small, 'arrive_near')
+    run(b_far, 'forward')
     run(b_out, 'arrive_near')
     run(a_out, 'drain')
     for item in b_out:
@@ -472,7 +480,7 @@
         ids_t, gate_t = ids.T, gate.T
         shape = jax.ShapeDtypeStruct
         between = [(RING, RING, n_tok, SPAN)] * 3 + per_part(RING, 2) * 2 + per_part(2) * 3
-        lanes = 4 + 3 + 2 + 1 + 3 + 3 + 3 + 3 * 6 + 3
+        lanes = 4 + 3 + 2 + 1 + 3 + 3 + 12 + 3 * 6 + 3
         return pl.pallas_call(
             functools.partial(layer_kernel, capacity),
             in_specs=[near] * 3 + [anywhere] * 2,

time: 315 us -> 315 us (level)
  no operation moved by 1% of the time
where the time goes in v9:
time: 315 us; the launch traced here: 314 us
  Pallas kernels  312 us (99%)
    pallas_call x1, Pallas kernels, local_step(): pl.pallas_call(functools.partial(layer_kernel, capacity), in_specs=[near]...  312 us

profile of v9, /device:TPU:1, one launch (start us, length us, event | category | flops | bytes accessed | tf_op | source)
XLA Modules:
  0.0 314.3 jit_solution(6287725015443842071)
XLA Ops:
  0.0 312.0 %layer.1 = (bf16[256,2048]{1,0:T(8,128)(2,1)}, bf16[4,4,256,768]{3,2,1,0:T(8,128)(2,1)}, bf16[4,4,256,768]{3,2,1,0:T(8,128)(2,1)}, bf16[4,4,256,768]{3,2,1,0:T(8...) custom-call(bf16[256,2048]{1,0:T(8,128)(2,1)} %refs_0_.1, ...), custom_call_target="tpu_custom_call" | custom-call | tf_op jit(solution)/shard_map/layer/pallas_call | solution.py:484
  312.0 2.3 copy.7

commit v10 on v9

--- a/solution.py
+++ b/solution.py
@@ -61,7 +61,7 @@
     def far(self):
         p = self.place
         for h, step in ((0, 1), (1, -1)):
-            self.start(self.source(p.pos(self.axis, 2), h), self.relay.at[h], h, h, p.core, p.at(self.axis, step))
+            self.start(self.source(p.pos(self.axis, 2), h), self.relay(h), h, h, p.core, p.at(self.axis, step))
 
     def near(self):
         p = self.place
@@ -76,9 +76,9 @@
     def forward(self):
         p = self.place
         for h, step in ((0, 1), (1, -1)):
-            self.landed(self.relay.at[h], h)
+            self.landed(self.relay(h), h)
             k, c, r = (p.core, h, 6 + p.core) if self.switch else (h, p.core, 6 + h)
-            self.start(self.relay.at[h], self.target(p.pos(self.axis, -step), k), 6 + h, r, c, p.at(self.axis, step))
+            self.start(self.relay(h), self.target(p.pos(self.axis, -step), k), 6 + h, r, c, p.at(self.axis, step))
 
     def arrive_near(self):
         p = self.place
@@ -143,13 +143,13 @@
 
     def add(self):
         for h, step in ((0, 1), (1, -1)):
-            self.landed(self.relay.at[h], h)
-            self.relay[h] += self.source(self.place.pos(self.axis, step), h)[...]
+            self.landed(self.relay(h), h)
+            self.relay(h)[...] += self.source(self.place.pos(self.axis, step), h)[...]
 
     def forward(self):
         p = self.place
         for h, step in ((0, 1), (1, -1)):
-            self.start(self.relay.at[h], self.target(h, h), 4 + h, 4 + h, p.core, p.at(self.axis, step))
+            self.start(self.relay(h), self.target(h, h), 4 + h, 4 + h, p.core, p.at(self.axis, step))
 
     def arrive(self):
         for side in (0, 1):
@@ -236,14 +236,24 @@
     b_out = [lane(Gather, second[r], lambda p, h, r=r, step=step: tokens[r].at[place.pos(first[r], step), pl.ds(h * half, half)],
                   lambda o, k, r=r, step=step: wide[r].at[o, place.pos(first[r], step), pl.ds(k * half, half)]) for step in (0, 1, 3, 2) for r in PARTS]
     b_own, b_near, b_far = b_out[:3], b_out[3:9], b_out[9:]
-    c_out = [lane(Lane, third[r], lambda p, h, i=3 * q + r: packed[i].at[p, h],
-                  lambda o, k, i=3 * q + r, r=r: rows[i].at[(k,) + spot(third[r], 'zyx', o)], c_relay[3 * q + r], True) for q, r in BOTH]
+    def along(axes, **index):
+        return tuple(index.get(axis, slice(None)) for axis in 'zyx' if axis in axes)
+
+    def c_piece(r, step):
+        b = place.pos(second[r], step)
+        return lane(Lane, third[r], lambda p, h: packed[r].at[(p, h) + along(ORDERS[r][:2], **{second[r]: b})],
+                    lambda o, k: rows[r].at[(k,) + along('zyx', **{second[r]: b, third[r]: o})], lambda h: c_relay[r].at[h, step], True)
+
+    c_own, c_near, c_far = [[c_piece(r, step) for step in steps for r in PARTS] for steps in ((0,), (1, 3), (2,))]
+    c_first = c_own + c_near + c_far
+    c_second = [lane(Lane, third[r], lambda p, h, r=r: packed[3 + r].at[p, h],
+                     lambda o, k, r=r: rows[3 + r].at[(k,) + spot(third[r], 'zyx', o)], lambda h, r=r: c_relay[3 + r].at[h], True) for r in PARTS]
     c_back = [lane(Lane, third[r], lambda p, h, i=3 * q + r, r=r: rows[i].at[(h,) + spot(third[r], 'zyx', p)],
-                   lambda o, k, i=3 * q + r: backs[i].at[o, k], cb_relay[3 * q + r]) for q, r in BOTH]
+                   lambda o, k, i=3 * q + r: backs[i].at[o, k], lambda h, i=3 * q + r: cb_relay[i].at[h]) for q, r in BOTH]
     b_back = [lane(Lane, second[r], lambda p, h, i=3 * q + r, r=r: backs[i].at[(slice(None), h) + spot(second[r], ORDERS[r][:2], p)],
-                   lambda o, k, i=3 * q + r: ends[i].at[o, k], bb_relay[3 * q + r], True) for q, r in BOTH]
+                   lambda o, k, i=3 * q + r: ends[i].at[o, k], lambda h, i=3 * q + r: bb_relay[i].at[h], True) for q, r in BOTH]
     a_back = [lane(Reduce, first[r], lambda p, h, r=r: sums[r].at[p, pl.ds(h * half, half)],
-                   lambda side, h, r=r: got[r].at[side, pl.ds(h * half, half)], sum_relay[r]) for r in PARTS]
+                   lambda side, h, r=r: got[r].at[side, pl.ds(h * half, half)], lambda h, r=r: sum_relay[r].at[h]) for r in PARTS]
     one, two = slice(0, 3), slice(3, 6)
 
     def pack(q, r, step, a):
@@ -363,6 +373,8 @@
     run(b_near, 'forward')
     run(b_small, 'arrive_near')
     run(b_far, 'forward')
+    run(c_own, 'far', 'near')
+    kept = own(c_own)
     run(b_out, 'arrive_near')
     run(a_out, 'drain')
     for item in b_out:
@@ -375,31 +387,35 @@
             loads[r].wait()
             pl.loop(0, RING)(lambda a, r=r: [pack(q, r, 1 + 2 * n, a) for q in STREAMS] and None)
 
+    run(c_near, 'far', 'near')
+    kept += own(c_near)
+    run(c_own, 'forward')
     run(b_small + [along_y], 'arrive_far')
     run([along_y], 'arrive_near')
     kept_z = own([along_z])
-    run([along_z], 'near')
     run(b_out, 'arrive_far')
     loads = slabs(2)
     for r in PARTS:
         loads[r].wait()
         pl.loop(0, RING)(lambda a, r=r: pack(0, r, 2, a))
-    run(c_out[one], 'far', 'near')
-    kept = own(c_out[one])
+    run([along_z], 'near')
+    run(c_far, 'far', 'near')
+    kept += own(c_far)
     for r in PARTS:
         pl.loop(0, RING)(lambda a, r=r: pack(1, r, 2, a))
-    run(c_out[one], 'forward')
-    run(c_out[two], 'far', 'near')
-    kept_two = own(c_out[two])
+    run(c_near, 'forward')
+    run(c_far, 'forward')
+    run(c_second, 'far', 'near')
+    kept_two = own(c_second)
     run([along_z], 'forward')
-    run(c_out[one], 'arrive')
+    run(c_first, 'arrive')
     wait(kept + weights)
     pl.loop(0, 2 * RING)(lambda n: expert(0, n))
     weights = [load(w_in.at[1], w_in_v, 2), load(w_out.at[1], w_out_v, 3)]
-    run(c_out[two], 'forward')
+    run(c_second, 'forward')
     run(c_back[one], 'far', 'near')
     kept = own(c_back[one])
-    run(c_out[two], 'arrive')
+    run(c_second, 'arrive')
     wait(kept_two + weights)
     pl.loop(0, 2 * RING)(lambda n: expert(1, n))
     run(c_back[one], 'forward')
@@ -416,7 +432,7 @@
     run(c_back[one], 'arrive')
     wait(kept)
     run(b_back[one], 'far', 'near')
-    run(c_out, 'drain')
+    run(c_first + c_second, 'drain')
     kept = own_rows(b_back[one], 0)
     for r in PARTS:
         sums[r][...] = jnp.zeros_like(sums[r])
@@ -480,7 +496,7 @@
         ids_t, gate_t = ids.T, gate.T
         shape = jax.ShapeDtypeStruct
         between = [(RING, RING, n_tok, SPAN)] * 3 + per_part(RING, 2) * 2 + per_part(2) * 3
-        lanes = 4 + 3 + 2 + 1 + 3 + 3 + 12 + 3 * 6 + 3
+        lanes = 4 + 3 + 2 + 1 + 3 + 3 + 12 + 12 + 3 + 2 * 6 + 3
         return pl.pallas_call(
             functools.partial(layer_kernel, capacity),
             in_specs=[near] * 3 + [anywhere] * 2,

time: 315 us -> 309 us (0.981)
  Pallas kernels: 312 us -> 306 us
    pallas_call x1, Pallas kernels: 312 us -> 306 us  [local_step(): pl.pallas_call(functools.partial(layer_kernel, capacity), in_specs=[near]...]
where the time goes in v10:
time: 309 us
  Pallas kernels  306 us (99%)
    pallas_call x1, Pallas kernels, local_step(): pl.pallas_call(functools.partial(layer_kernel, capacity), in_specs=[near]...  306 us

profile of v10, /device:TPU:1, one launch (start us, length us, event | category | flops | bytes accessed | tf_op | source)
XLA Modules:
  0.0 308.7 jit_solution(3873678228882251103)
XLA Ops:
  0.0 306.4 %layer.1 = (bf16[256,2048]{1,0:T(8,128)(2,1)}, bf16[4,4,256,768]{3,2,1,0:T(8,128)(2,1)}, bf16[4,4,256,768]{3,2,1,0:T(8,128)(2,1)}, bf16[4,4,256,768]{3,2,1,0:T(8...) custom-call(bf16[256,2048]{1,0:T(8,128)(2,1)} %refs_0_.1, ...), custom_call_target="tpu_custom_call" | custom-call | tf_op jit(solution)/shard_map/layer/pallas_call | solution.py:500
  306.4 2.3 copy.7
